TPU v7x, 32 devices: a whole 2x2x4 slice. The times are simulated.
32 devices in a mesh: section: 4 (over y, core), dp: 8 (over z, x).
Axes of the slice: x: 2, y: 2, z: 4, core: 2. Of those that a mesh axis runs over, the one named last changes fastest.
Arguments:
- acts: bfloat16 [4, 4096, 3584], P('section', 'dp'), may hold values from -400 to 400
- cotangent: bfloat16 [4096, 3584], P('dp'), may hold values from -6 to 6
- frozen: bfloat16 [4, 3584, 3584], P('section', 'dp'), may hold values from -0.09375 to 0.09375
- down_adapter: bfloat16 [4, 16, 3584], P('section'), may hold values from -0.25 to 0.25
- up_adapter: bfloat16 [4, 16, 3584], P('section'), may hold values from -0.25 to 0.25
- example_ids: int32 [8, 4], P('dp'), may hold values from 0 to 3, each once within a row
- lengths: int32 [8, 4], P('dp'), may hold values from 32 to 128
Outputs:
- grad_down: float32 [4, 16, 3584], P('section', None, 'dp')
- grad_up: float32 [4, 16, 3584], P('section', None, 'dp')
- example_norms: float32 [8, 4], P('dp')
Inputs may be any that keep to these rules, and one draw needn't show every extreme that they name: `example_ids`: each row is an ordering of the 4 examples of one replica.
All inputs are finite; a program needn't handle non-finite values.
Results may differ from a plain program's by a relative error of at most 0.009.
Values may be sent and summed in bfloat16 or wider, within the bound.
No kernel may reach another device: no remote copies, remote signals or barrier semaphores. Data moves between devices by JAX's collectives and lax.ppermute only.
A program may use at most 128 MiB of HBM per device.

v0:
```python
import math

import jax
import jax.numpy as jnp
from jax import lax
from jax.sharding import PartitionSpec as P


def from_behind(value, axis, steps):
    count = lax.axis_size(axis)
    first, last = (max(0, -steps), min(count, count - steps))
    return lax.ppermute(value, axis, [(source, source + steps) for source in range(first, last)])


def on_device(acts, cotangent, frozen, down_adapter, up_adapter, example_ids, lengths):
    section_count = lax.axis_size("section")
    section_index = lax.axis_index("section")
    replica_count = lax.axis_size("dp")
    layer_inputs = acts[0]
    down_rows = down_adapter[0]
    up_rows = up_adapter[0]
    slot_count = example_ids.shape[1]
    positions = layer_inputs.shape[0] // slot_count
    features = layer_inputs.shape[1]
    rank_size = down_rows.shape[0]
    choose = (example_ids[0][:, None] == jnp.arange(slot_count, dtype=jnp.int32)[None, :]).astype(
        jnp.int32
    )
    slot_length = jnp.sum(choose * lengths[0][None, :], axis=1)
    live_mask = (jnp.arange(positions, dtype=jnp.int32)[None, :] < slot_length[:, None]).astype(
        jnp.bfloat16
    )
    seeded = cotangent.reshape(slot_count, positions, features) * live_mask[:, :, None]
    input_blocks = layer_inputs.reshape(slot_count, positions, features)
    clip_scale = math.sqrt(2.0 * rank_size * features) / math.sqrt(replica_count * slot_count)
    weight = lax.all_gather(frozen[0], "dp", axis=0, tiled=True)

    def backstep(out_grad):
        up_grad = jnp.dot(out_grad, up_rows.T, preferred_element_type=jnp.float32).astype(
            jnp.bfloat16
        )
        in_grad = jnp.dot(out_grad, weight.T, preferred_element_type=jnp.float32)
        in_grad = in_grad + jnp.dot(up_grad, down_rows, preferred_element_type=jnp.float32)
        return in_grad.astype(jnp.bfloat16)

    def local_terms(out_grad, inputs):
        up_grad = jnp.dot(out_grad, up_rows.T, preferred_element_type=jnp.float32).astype(
            jnp.bfloat16
        )
        down_act = jnp.dot(inputs, down_rows.T, preferred_element_type=jnp.float32).astype(
            jnp.bfloat16
        )
        down_term = jnp.dot(up_grad.T, inputs, preferred_element_type=jnp.float32)
        up_term = jnp.dot(down_act.T, out_grad, preferred_element_type=jnp.float32)
        input_gram = jnp.dot(inputs, inputs.T, preferred_element_type=jnp.float32)
        upgrad_gram = jnp.dot(up_grad, up_grad.T, preferred_element_type=jnp.float32)
        act_gram = jnp.dot(down_act, down_act.T, preferred_element_type=jnp.float32)
        outgrad_gram = jnp.dot(out_grad, out_grad.T, preferred_element_type=jnp.float32)
        square_sum = jnp.sum(input_gram * upgrad_gram) + jnp.sum(act_gram * outgrad_gram)
        return (square_sum, down_term, up_term)

    tick_count = slot_count + section_count - 1
    incoming = jnp.zeros((positions, features), jnp.bfloat16)
    stored_grads = jnp.zeros((slot_count, positions, features), jnp.bfloat16)
    sum_down = jnp.zeros((rank_size, features), jnp.float32)
    sum_up = jnp.zeros((rank_size, features), jnp.float32)
    slot_norms = jnp.zeros((slot_count,), jnp.float32)

    def tick_step(tick, carry):
        incoming, stored_grads, sum_down, sum_up, slot_norms = carry
        micro_index = tick - (section_count - 1 - section_index)
        active = (micro_index >= 0) & (micro_index < slot_count)
        held_index = jnp.clip(micro_index, 0, slot_count - 1)
        fresh = lax.dynamic_index_in_dim(seeded, held_index, 0, keepdims=False)
        start = jnp.where(section_index == section_count - 1, fresh, incoming)
        produced = lax.cond(active, backstep, lambda value: jnp.zeros_like(value), start)
        previous = lax.dynamic_index_in_dim(stored_grads, held_index, 0, keepdims=False)
        kept = jnp.where(active, start, previous)
        stored_grads = lax.dynamic_update_index_in_dim(stored_grads, kept, held_index, 0)
        incoming = from_behind(produced, "section", -1)
        return (incoming, stored_grads, sum_down, sum_up, slot_norms)

    carry = (incoming, stored_grads, sum_down, sum_up, slot_norms)
    incoming, stored_grads, sum_down, sum_up, slot_norms = lax.fori_loop(
        0, tick_count, tick_step, carry
    )
    square_sums, down_terms, up_terms = jax.vmap(local_terms)(stored_grads, input_blocks)
    totals = lax.psum(square_sums, "section")
    slot_norms = jnp.sqrt(totals)
    factors = clip_scale / (slot_norms + 0.01)
    sum_down = jnp.sum(factors[:, None, None] * down_terms, axis=0)
    sum_up = jnp.sum(factors[:, None, None] * up_terms, axis=0)
    grad_down, grad_up = (
        lax.psum_scatter(sum_down, "dp", scatter_dimension=1, tiled=True),
        lax.psum_scatter(sum_up, "dp", scatter_dimension=1, tiled=True),
    )
    example_norms = jnp.sum(choose.astype(jnp.float32) * slot_norms[:, None], axis=0)
    return (grad_down[None], grad_up[None], example_norms[None])


def solution(mesh):
    in_specs = (
        P("section", "dp", None),
        P("dp", None),
        P("section", "dp", None),
        P("section", None, None),
        P("section", None, None),
        P("dp", None),
        P("dp", None),
    )
    out_specs = (P("section", None, "dp"), P("section", None, "dp"), P("dp", None))
    return jax.shard_map(
        on_device, mesh=mesh, in_specs=in_specs, out_specs=out_specs, check_vma=False
    )
```

profile of v0, /device:TPU:0, one launch (start us, length us, event | category | flops | bytes accessed | tf_op | source)
XLA Modules:
  0.0 877.4 jit_solution(13300628261146908714)
XLA Ops:
  9.0 3.1 convolution_convert_fusion.1
  14.5 487.9 %all-gather.3.cloned.1.call-done = bf16[1,3584,3584]{2,1,0:T(8,128)(2,1)} async-done(((bf16[1,448,3584]{2,1,0:T(8,128)(2,1)}), bf16[1,3584,3584]{2,1,0:T(8,128)(2,1)}) %all-gather.3.cloned.1.call-update) | async-done | bytes 25690128 | tf_op jit(solution)/shard_map/all_gather | solution.py:36
  504.6 203.7 %while.17 = (s32[]{:T(128)}, bf16[128,3584]{1,0:T(8,128)(2,1)S(1)}, bf16[4,128,3584]{2,1,0:T(8,128)(2,1)}, s32[]{:T(128)}, pred[]{:T(512)}, /*index=5*/bf16[4,12...) while((s32[]{:T(128)}, bf16[128,3584]{1,0:T(8,128)(2,1)S(1)}, ...), condition=%wide.region_4.5_spmd, body=%wide.region_1.4_spmd.sunk | while | flops 3319531520 | bytes 42435348 | solution.py:84
  505.9 2.6 bitcast_dynamic-update-slice_fusion.2
  510.8 3.3 collective-permute-done
  515.4 2.6 bitcast_dynamic-update-slice_fusion.2
  520.3 13.0 %collective-permute-done = bf16[128,3584]{1,0:T(8,128)(2,1)S(1)} collective-permute-done((bf16[128,3584]{1,0:T(8,128)(2,1)}, bf16[128,3584]{1,0:T(8,128)(2,1)S(1)}, u32[]{:S(2)}, u32[]{:S(2)}) %collective-permute-start) | collective-permute-done | bytes 917536 | tf_op jit(solution)/shard_map/while/body/eval_jaxpr/ppermute | solution.py:12
  534.5 2.6 bitcast_dynamic-update-slice_fusion.2
  539.4 44.0 %collective-permute-done = bf16[128,3584]{1,0:T(8,128)(2,1)S(1)} collective-permute-done((bf16[128,3584]{1,0:T(8,128)(2,1)}, bf16[128,3584]{1,0:T(8,128)(2,1)S(1)}, u32[]{:S(2)}, u32[]{:S(2)}) %collective-permute-start) | collective-permute-done | bytes 917536 | tf_op jit(solution)/shard_map/while/body/eval_jaxpr/ppermute | solution.py:12
  584.7 2.6 bitcast_dynamic-update-slice_fusion.2
  587.3 15.1 %conditional.2 = (bf16[128,3584]{1,0:T(8,128)(2,1)}) conditional(s32[]{:T(128)} %convert_element_type.49, () %tuple.51, (bf16[128,3584]{1,0:T(8,128)(2,1)S(1)}, bf16[3584,3584]{1,0:T(8,128)(2,1)}, bf16[16,3584]{1,0:T(8,128)(2,1)S(1)}, bf16[16,3584]{1,0:T(8,128)(2,1)S(1)}) %tuple.52), branch_computations={%region_2.2_spmd, %region_3.3_spmd} | conditional | flops 3318614016 | bytes 32342024 | solution.py:76
  587.3 12.9 %fusion.9 = f32[128,3584]{1,0:T(8,128)S(1)} fusion(bf16[128,3584]{1,0:T(8,128)(2,1)S(1)} %get-tuple-element.202, bf16[3584,3584]{1,0:T(8,128)(2,1)} %get-tuple-element.203), kind=kOutput, calls=%fused_computation.27 | convolution fusion | flops 3288334336 | bytes 28442624 | tf_op jit(solution)/shard_map/while/body/eval_jaxpr/cond/branch_1_fun/dot_general | solution.py:42
  600.2 2.2 fusion
  603.7 13.6 %collective-permute-done = bf16[128,3584]{1,0:T(8,128)(2,1)S(1)} collective-permute-done((bf16[128,3584]{1,0:T(8,128)(2,1)}, bf16[128,3584]{1,0:T(8,128)(2,1)S(1)}, u32[]{:S(2)}, u32[]{:S(2)}) %collective-permute-start) | collective-permute-done | bytes 917536 | tf_op jit(solution)/shard_map/while/body/eval_jaxpr/ppermute | solution.py:12
  618.5 2.6 bitcast_dynamic-update-slice_fusion.2
  621.1 15.1 %conditional.2 = (bf16[128,3584]{1,0:T(8,128)(2,1)}) conditional(s32[]{:T(128)} %convert_element_type.49, () %tuple.51, (bf16[128,3584]{1,0:T(8,128)(2,1)S(1)}, bf16[3584,3584]{1,0:T(8,128)(2,1)}, bf16[16,3584]{1,0:T(8,128)(2,1)S(1)}, bf16[16,3584]{1,0:T(8,128)(2,1)S(1)}) %tuple.52), branch_computations={%region_2.2_spmd, %region_3.3_spmd} | conditional | flops 3318614016 | bytes 32342024 | solution.py:76
  621.1 12.9 %fusion.9 = f32[128,3584]{1,0:T(8,128)S(1)} fusion(bf16[128,3584]{1,0:T(8,128)(2,1)S(1)} %get-tuple-element.202, bf16[3584,3584]{1,0:T(8,128)(2,1)} %get-tuple-element.203), kind=kOutput, calls=%fused_computation.27 | convolution fusion | flops 3288334336 | bytes 28442624 | tf_op jit(solution)/shard_map/while/body/eval_jaxpr/cond/branch_1_fun/dot_general | solution.py:42
  637.5 13.6 %collective-permute-done = bf16[128,3584]{1,0:T(8,128)(2,1)S(1)} collective-permute-done((bf16[128,3584]{1,0:T(8,128)(2,1)}, bf16[128,3584]{1,0:T(8,128)(2,1)S(1)}, u32[]{:S(2)}, u32[]{:S(2)}) %collective-permute-start) | collective-permute-done | bytes 917536 | tf_op jit(solution)/shard_map/while/body/eval_jaxpr/ppermute | solution.py:12
  652.3 2.6 bitcast_dynamic-update-slice_fusion.2
  654.9 15.1 %conditional.2 = (bf16[128,3584]{1,0:T(8,128)(2,1)}) conditional(s32[]{:T(128)} %convert_element_type.49, () %tuple.51, (bf16[128,3584]{1,0:T(8,128)(2,1)S(1)}, bf16[3584,3584]{1,0:T(8,128)(2,1)}, bf16[16,3584]{1,0:T(8,128)(2,1)S(1)}, bf16[16,3584]{1,0:T(8,128)(2,1)S(1)}) %tuple.52), branch_computations={%region_2.2_spmd, %region_3.3_spmd} | conditional | flops 3318614016 | bytes 32342024 | solution.py:76
  654.9 12.9 %fusion.9 = f32[128,3584]{1,0:T(8,128)S(1)} fusion(bf16[128,3584]{1,0:T(8,128)(2,1)S(1)} %get-tuple-element.202, bf16[3584,3584]{1,0:T(8,128)(2,1)} %get-tuple-element.203), kind=kOutput, calls=%fused_computation.27 | convolution fusion | flops 3288334336 | bytes 28442624 | tf_op jit(solution)/shard_map/while/body/eval_jaxpr/cond/branch_1_fun/dot_general | solution.py:42
  671.3 13.6 %collective-permute-done = bf16[128,3584]{1,0:T(8,128)(2,1)S(1)} collective-permute-done((bf16[128,3584]{1,0:T(8,128)(2,1)}, bf16[128,3584]{1,0:T(8,128)(2,1)S(1)}, u32[]{:S(2)}, u32[]{:S(2)}) %collective-permute-start) | collective-permute-done | bytes 917536 | tf_op jit(solution)/shard_map/while/body/eval_jaxpr/ppermute | solution.py:12
  686.1 2.6 bitcast_dynamic-update-slice_fusion.2
  688.7 15.1 %conditional.2 = (bf16[128,3584]{1,0:T(8,128)(2,1)}) conditional(s32[]{:T(128)} %convert_element_type.49, () %tuple.51, (bf16[128,3584]{1,0:T(8,128)(2,1)S(1)}, bf16[3584,3584]{1,0:T(8,128)(2,1)}, bf16[16,3584]{1,0:T(8,128)(2,1)S(1)}, bf16[16,3584]{1,0:T(8,128)(2,1)S(1)}) %tuple.52), branch_computations={%region_2.2_spmd, %region_3.3_spmd} | conditional | flops 3318614016 | bytes 32342024 | solution.py:76
  688.7 12.9 %fusion.9 = f32[128,3584]{1,0:T(8,128)S(1)} fusion(bf16[128,3584]{1,0:T(8,128)(2,1)S(1)} %get-tuple-element.202, bf16[3584,3584]{1,0:T(8,128)(2,1)} %get-tuple-element.203), kind=kOutput, calls=%fused_computation.27 | convolution fusion | flops 3288334336 | bytes 28442624 | tf_op jit(solution)/shard_map/while/body/eval_jaxpr/cond/branch_1_fun/dot_general | solution.py:42
  705.1 3.3 collective-permute-done
  708.4 3.2 convolution_convert_fusion.2
  715.1 12.7 %psum.7 = f32[4]{0:T(128)S(1)} all-reduce(f32[4]{0:T(128)S(1)} %add.41), channel_id=1, replica_groups=mesh['section'=4,'dp'=8] {'section'}, use_global_device_ids=true, to_apply=%region_7.8 | all-reduce | flops 4 | bytes 32 | tf_op jit(solution)/shard_map/psum | solution.py:88
  727.9 2.6 fusion.2
  732.4 2.6 fusion.1
  737.5 62.1 %reduce-scatter.9.cloned.1.call-done = f32[448,16]{1,0:T(8,128)} async-done(((f32[3584,16]{1,0:T(8,128)}), f32[448,16]{1,0:T(8,128)}) %reduce-scatter.9.cloned.1.call-update) | async-done | bytes 28688
  801.3 68.0 %reduce-scatter.7.cloned.1.call-done = f32[448,16]{1,0:T(8,128)} async-done(((f32[3584,16]{1,0:T(8,128)}), f32[448,16]{1,0:T(8,128)}) %reduce-scatter.7.cloned.1.call-update) | async-done | bytes 28688
  (57 shorter events, 47.7 us)
Async XLA Ops:
  7.2 495.3 %all-gather.3.cloned.1.call-start = ((), (), s32[]{:S(2)}) async-start(), calls=%async_computation.2 | async-start | bytes 28901376 | tf_op jit(solution)/shard_map/all_gather | solution.py:36
  7.9 791.7 %reduce-scatter.9.cloned.1.call-start = ((), (), s32[]{:S(2)}) async-start(), calls=%async_computation.4 | async-start | bytes 2064384
  8.0 4.5 copy-start.4
  14.5 490.1 %copy-start.2 = (bf16[1,16,3584]{2,1,0:T(8,128)(2,1)S(1)}, bf16[1,16,3584]{2,1,0:T(8,128)(2,1)}, u32[]{:S(2)}) copy-start(bf16[1,16,3584]{2,1,0:T(8,128)(2,1)} %param.14) | copy-start | bytes 344068
  14.5 490.1 %copy-start.3 = (bf16[1,16,3584]{2,1,0:T(8,128)(2,1)S(1)}, bf16[1,16,3584]{2,1,0:T(8,128)(2,1)}, u32[]{:S(2)}) copy-start(bf16[1,16,3584]{2,1,0:T(8,128)(2,1)} %param.15) | copy-start | bytes 344068
  509.5 4.6 collective-permute-start
  519.0 14.3 %collective-permute-start = (bf16[128,3584]{1,0:T(8,128)(2,1)}, bf16[128,3584]{1,0:T(8,128)(2,1)S(1)}, u32[]{:S(2)}, u32[]{:S(2)}) collective-permute-start(bf16[128,3584]{1,0:T(8,128)(2,1)} %get-tuple-element.341), channel_id=1, source_target_pairs={{8,0},{16,8},{24,16},{9,1},{17,9},{25,17},{10,2},{18,10},{26,18},{... | collective-permute-start | bytes 2752520 | tf_op jit(solution)/shard_map/while/body/eval_jaxpr/ppermute | solution.py:12
  538.1 45.3 %collective-permute-start = (bf16[128,3584]{1,0:T(8,128)(2,1)}, bf16[128,3584]{1,0:T(8,128)(2,1)S(1)}, u32[]{:S(2)}, u32[]{:S(2)}) collective-permute-start(bf16[128,3584]{1,0:T(8,128)(2,1)} %get-tuple-element.341), channel_id=1, source_target_pairs={{8,0},{16,8},{24,16},{9,1},{17,9},{25,17},{10,2},{18,10},{26,18},{... | collective-permute-start | bytes 2752520 | tf_op jit(solution)/shard_map/while/body/eval_jaxpr/ppermute | solution.py:12
  602.4 14.9 %collective-permute-start = (bf16[128,3584]{1,0:T(8,128)(2,1)}, bf16[128,3584]{1,0:T(8,128)(2,1)S(1)}, u32[]{:S(2)}, u32[]{:S(2)}) collective-permute-start(bf16[128,3584]{1,0:T(8,128)(2,1)} %get-tuple-element.341), channel_id=1, source_target_pairs={{8,0},{16,8},{24,16},{9,1},{17,9},{25,17},{10,2},{18,10},{26,18},{... | collective-permute-start | bytes 2752520 | tf_op jit(solution)/shard_map/while/body/eval_jaxpr/ppermute | solution.py:12
  636.2 14.9 %collective-permute-start = (bf16[128,3584]{1,0:T(8,128)(2,1)}, bf16[128,3584]{1,0:T(8,128)(2,1)S(1)}, u32[]{:S(2)}, u32[]{:S(2)}) collective-permute-start(bf16[128,3584]{1,0:T(8,128)(2,1)} %get-tuple-element.341), channel_id=1, source_target_pairs={{8,0},{16,8},{24,16},{9,1},{17,9},{25,17},{10,2},{18,10},{26,18},{... | collective-permute-start | bytes 2752520 | tf_op jit(solution)/shard_map/while/body/eval_jaxpr/ppermute | solution.py:12
  670.0 14.9 %collective-permute-start = (bf16[128,3584]{1,0:T(8,128)(2,1)}, bf16[128,3584]{1,0:T(8,128)(2,1)S(1)}, u32[]{:S(2)}, u32[]{:S(2)}) collective-permute-start(bf16[128,3584]{1,0:T(8,128)(2,1)} %get-tuple-element.341), channel_id=1, source_target_pairs={{8,0},{16,8},{24,16},{9,1},{17,9},{25,17},{10,2},{18,10},{26,18},{... | collective-permute-start | bytes 2752520 | tf_op jit(solution)/shard_map/while/body/eval_jaxpr/ppermute | solution.py:12
  703.8 4.6 collective-permute-start
  708.4 3.5 copy-start.1
  711.9 2.0 copy-start
  732.3 4.5 copy-start.5
  732.4 136.9 %reduce-scatter.7.cloned.1.call-start = ((), (), s32[]{:S(2)}) async-start(), calls=%async_computation.3 | async-start | bytes 2064384
Sparse Core Ops, SparseCore 0:
  9.5 492.9 all-gather.2
  732.5 67.0 reduce-scatter.8
  803.1 66.1 reduce-scatter.6
where the time goes:
time: 878 us; the launch traced here: 877 us
  waiting for transfers between devices  723 us (82%)
  matrix products  74.9 us (9%)
  other arithmetic  21.9 us (2%)
  local copies, waits for them, and re-layouts  21.6 us (2%)
  between operations  13.9 us (2%)
  blocking collectives  12.7 us (1%)
  starting transfers between devices  9.08 us (1%)
    all_gather x1, waiting for transfers between devices, on_device(): weight = lax.all_gather(frozen[0], 'dp', axis=0, tiled=True)  488 us
    unnamed x5, waiting for transfers between devices  131 us
    ppermute x7, waiting for transfers between devices, from_behind(): lax.ppermute(value, axis, [(source, source + steps) for source in range(f...  104 us
    dot_general x4, matrix products, backstep(): in_grad = jnp.dot(out_grad, weight.T, preferred_element_type=jnp.float32)  51.6 us
    dynamic_update_slice x7, other arithmetic, tick_step(): lax.dynamic_update_index_in_dim(stored_grads, kept, held_index, 0)  18.2 us
  transfers between devices with their start and end apart: 10, of which 10 were waited for; matrix products, arithmetic and copies ran while one was open for 2% of the time, Pallas kernels for 0%

commit v1 on v0

v1 whole, which is shorter than its diff:
```python
import math

import jax
import jax.numpy as jnp
from jax import lax
from jax.experimental import pallas as pl
from jax.experimental.pallas import tpu as pltpu
from jax.sharding import Mesh, PartitionSpec as P

LANES = 128
BF16 = jnp.bfloat16
F32 = jnp.float32
VMEM = pl.BlockSpec(memory_space=pltpu.VMEM)
SMEM = pl.BlockSpec(memory_space=pltpu.SMEM)


def mm(left, right, dims):
    return lax.dot_general(left, right, (dims, ((), ())), preferred_element_type=F32)


def nt(left, right):
    return mm(left, right, ((1,), (1,)))


def nn(left, right):
    return mm(left, right, ((1,), (0,)))


def local_call(body, where, arrays, shapes, scratch=(), specs=None):
    specs = [VMEM] * len(arrays) if specs is None else specs
    return pl.pallas_call(
        body,
        out_shape=shapes,
        grid=(1,),
        in_specs=[SMEM] + specs,
        out_specs=[VMEM] * len(shapes),
        scratch_shapes=list(scratch),
        compiler_params=pltpu.CompilerParams(vmem_limit_bytes=56 * 1024 * 1024),
    )(where, *arrays)


def shape_of(dims, dtype=BF16):
    return jax.ShapeDtypeStruct(dims, dtype)


def xor_permute(value, axes, count, step):
    return lax.ppermute(value, axes, [(i, i ^ step) for i in range(count)])


class Plan:
    def __init__(self, sizes, features, rank, slots, positions, block):
        self.ny, self.nc, self.nz, self.nx = sizes
        self.sections, self.replicas = self.ny * self.nc, self.nz * self.nx
        self.quarters = self.ny * self.nx
        self.features, self.rank, self.slots, self.positions = features, rank, slots, positions
        self.block = block
        self.part = features // self.nz
        self.width = -(-self.part // (self.quarters * LANES)) * LANES
        self.wide = self.nz * self.width
        self.half = slots // self.nc
        self.group = self.half * rank
        self.height = self.group * self.replicas

    def window(self, replica):
        low = replica * self.block // LANES * LANES
        return low, min(-(-self.block // LANES) * LANES, self.features - low)

    def lane(self, quarter, step):
        low = quarter * self.width + step * LANES
        return jnp.minimum(low, self.part - LANES), low < self.part


def cut_weight(plan, where, weight_ref, *outs):
    quarter, iz = where[0], where[1]
    for k, out in enumerate(outs):
        for m in range(plan.nz):
            for h in range(plan.width // LANES):
                low, _ = plan.lane(quarter ^ k, h)
                start = pl.multiple_of((iz ^ m) * plan.part + low, LANES)
                lanes = slice(m * plan.width + h * LANES, m * plan.width + (h + 1) * LANES)
                out[:, lanes] = weight_ref[:, pl.ds(start, LANES)]


def sort_adapters(plan, where, *refs):
    quarter, iz, section = where[0], where[1], where[2]
    ins, (up_quarter, up_part, down_part) = refs[: plan.sections], refs[plan.sections :]
    for j, known in enumerate(ins):
        s = section ^ j
        for m in range(plan.nz):
            for h in range(plan.width // LANES):
                low, _ = plan.lane(quarter, h)
                start = pl.multiple_of((iz ^ m) * plan.part + low, LANES)
                lanes = slice(m * plan.width + h * LANES, m * plan.width + (h + 1) * LANES)
                up_quarter[s, :, lanes] = known[:, pl.ds(start, LANES)]
        start = pl.multiple_of(iz * plan.part, LANES)
        up_part[s] = known[:, pl.ds(start, plan.part)]
        down_part[s] = known[:, plan.features :]


def collect(plan, where, *refs):
    for k in range(plan.quarters):
        refs[plan.quarters][where[0] ^ k] = refs[k][...]


def first_rows(plan, where, *refs):
    iz, section, iy, ic, ix, replica = where[1], where[2], where[3], where[4], where[5], where[6]
    tokens = plan.slots * plan.positions
    known_acts = refs[: plan.sections]
    grad, weight, up_rows, own_down, low_out, high_out, act, rows, seeds = refs[plan.sections :]
    for j, known in enumerate(known_acts):
        act[section ^ j] = known[...]
    for i in range(plan.half):
        start = pl.multiple_of((ic * plan.half + i) * plan.positions, plan.positions)
        left = jnp.concatenate([act[s, :, pl.ds(start, plan.positions)] for s in range(plan.sections - 1)], axis=0)
        for m in range(plan.nz):
            lanes = pl.multiple_of((iz ^ m) * plan.part, LANES)
            right = grad[pl.ds(start, plan.positions), pl.ds(lanes, plan.part)]
            made = nn(left, right).astype(BF16)
            for s in range(plan.sections - 1):
                low = s * plan.group + i * plan.rank
                rows[m, low : low + plan.rank, :] = made[s * plan.rank : (s + 1) * plan.rank]
    start_rows = act[0, :, tokens : tokens + plan.block]
    seed = nn(start_rows, weight[...]) + nn(nt(start_rows, own_down[...]).astype(BF16), up_rows[...])
    seeds[...] = seed.astype(BF16)
    for d in range(plan.replicas):
        low, window = plan.window(d)
        low_out[d, plan.group :, :window] = seeds[:, low : low + window]
    for kx in range(plan.nx):
        quarter = iy * plan.nx + (ix ^ kx)
        for m in range(plan.nz):
            for h in range(plan.width // LANES):
                low, there = plan.lane(quarter, h)
                tile = rows[m, :, pl.ds(pl.multiple_of(low, LANES), LANES)]
                tile = jnp.where(there, tile, jnp.zeros_like(tile))
                for kz in range(plan.nz):
                    at = (kz ^ m) * plan.width + h * LANES
                    there_index = replica ^ (kz * plan.nx + kx)
                    low_out[there_index, : plan.group, at : at + LANES] = tile[: plan.group]
                    high_out[there_index, :, at : at + LANES] = tile[plan.group :]


def stage_rows(plan, t, count, where, *refs):
    quarter, ic = where[0], where[4]
    pieces = refs[:count]
    mine, twin, up_quarter, down_part = refs[count : count + 4]
    outs = refs[count + 4 : count + 4 + plan.quarters]
    flat, made = refs[count + 4 + plan.quarters :]
    if count == 1:
        flat = pieces[0]
    else:
        for j, piece in enumerate(pieces):
            flat[:, j * plan.width : (j + 1) * plan.width] = piece[...]
    tall = plan.height

    def compute(held):
        def tile(index, carry):
            at = pl.ds(pl.multiple_of(index * tall, tall), tall)
            rows = flat[at, :]
            bend = nt(rows, up_quarter[t]).astype(BF16)
            matrix = held[...].reshape(plan.part, plan.wide)
            for q in range(plan.quarters):
                low, high = min(q * plan.width, plan.part), min((q + 1) * plan.width, plan.part)
                if high > low:
                    value = nt(rows, matrix[low:high]) + nn(bend, down_part[t, :, low:high])
                    made[quarter ^ q, at, : high - low] = value.astype(BF16)
                if high - low < plan.width:
                    made[quarter ^ q, at, high - low :] = jnp.zeros((tall, plan.width - (high - low)), BF16)
            return carry

        lax.fori_loop(0, flat.shape[0] // tall, tile, 0)

    @pl.when(ic == t % plan.nc)
    def _():
        compute(mine)

    @pl.when(ic != t % plan.nc)
    def _():
        compute(twin)

    for k, out in enumerate(outs):
        out[...] = made[k]


def carry_rows(plan, t, count, split, where, *refs):
    quarter, ic = where[0], where[4]
    pieces = refs[:count]
    mine, twin, up_quarter, up_part, down_part = refs[count : count + 5]
    outs = refs[count + 5 : -1]
    stacked = refs[-1]
    old = (t - 1) * plan.rank
    if count == 1:
        stacked[:old, : plan.part] = pieces[0][...]
    else:
        for k, piece in enumerate(pieces):
            start = pl.multiple_of((quarter ^ k) * plan.width, LANES)
            stacked[:old, pl.ds(start, plan.width)] = piece[...]
    stacked[old:, : plan.part] = up_part[t - 1]

    def compute(held):
        rows = stacked[:, : plan.part]
        bend = nt(rows, down_part[t]).astype(BF16)
        value = nn(rows, held[...].reshape(plan.part, plan.wide)) + nn(bend, up_quarter[t])
        value = value.astype(BF16)
        if split:
            for m, out in enumerate(outs):
                out[...] = value[:, m * plan.width : (m + 1) * plan.width]
        else:
            outs[0][...] = value

    @pl.when(ic == t % plan.nc)
    def _():
        compute(mine)

    @pl.when(ic != t % plan.nc)
    def _():
        compute(twin)


def own_terms(plan, where, *refs):
    quarter, iz, section = where[0], where[1], where[2]
    pieces = refs[: plan.quarters]
    up_rows, grad, inputs, live, act = refs[plan.quarters : plan.quarters + 5]
    down_terms, top_terms, squares, carried = refs[plan.quarters + 5 :]
    last = section == plan.sections - 1
    for k, piece in enumerate(pieces):
        for m in range(plan.nz):
            for h in range(plan.width // LANES):
                low, there = plan.lane(quarter ^ k, h)
                start = pl.multiple_of((iz ^ m) * plan.part + low, LANES)

                @pl.when(there)
                def _():
                    at = m * plan.width + h * LANES
                    carried[:, pl.ds(start, LANES)] = piece[:, at : at + LANES]

    @pl.when(last)
    def _():
        carried[...] = up_rows[...]

    up_grad = (nt(carried[...], grad[...]).astype(BF16).astype(F32) * live[...]).astype(BF16)
    for m in range(plan.slots):
        where_rows = slice(m * plan.positions, (m + 1) * plan.positions)
        down = nn(up_grad[:, where_rows], inputs[where_rows, :])
        top = nn(act[:, where_rows], grad[where_rows, :])
        down_terms[m] = down
        top_terms[m] = top
        total = jnp.sum(down * down) + jnp.where(last, jnp.sum(top * top), 0.0)
        squares[m : m + 1, :] = jnp.full((1, LANES), total, F32)


def on_device(acts, cotangent, frozen, down_adapter, up_adapter, example_ids, lengths):
    sizes = [lax.axis_size(name) for name in ("y", "c", "z", "x")]
    ny, nc, nz, nx = sizes
    iy, ic, iz, ix = (lax.axis_index(name) for name in ("y", "c", "z", "x"))
    inputs, weight = acts[0], frozen[0]
    down_rows, up_rows = down_adapter[0], up_adapter[0]
    slots = example_ids.shape[1]
    tokens, features = inputs.shape
    positions, rank, block = tokens // slots, down_rows.shape[0], weight.shape[0]
    plan = Plan(sizes, features, rank, slots, positions, block)
    sections, replicas, quarters = plan.sections, plan.replicas, plan.quarters
    part, width, wide, half = plan.part, plan.width, plan.wide, plan.half
    section = iy * nc + ic
    quarter = iy * nx + ix
    replica = iz * nx + ix
    where = jnp.stack([quarter, iz, section, iy, ic, ix, replica]).astype(jnp.int32)
    last = section == sections - 1

    def run(body, arrays, shapes, scratch=(), specs=None, extra=(), after=()):
        def kernel(at, *refs):
            body(plan, *extra, at, *refs[len(after) :])

        specs = [VMEM] * len(arrays) if specs is None else specs
        specs = [pl.BlockSpec(memory_space=pl.ANY)] * len(after) + specs
        arrays = list(after) + list(arrays)
        return local_call(kernel, where, arrays, shapes, scratch, specs)

    choose = (example_ids[0][:, None] == jnp.arange(slots, dtype=jnp.int32)[None, :]).astype(jnp.int32)
    slot_length = jnp.sum(choose * lengths[0][None, :], axis=1)
    live = jnp.arange(positions, dtype=jnp.int32)[None, :] < slot_length[:, None]
    live = live.astype(F32).reshape(1, tokens)
    clip_scale = math.sqrt(2.0 * rank * features) / math.sqrt(replicas * slots)

    down_act = (nt(down_rows, inputs).astype(BF16).astype(F32) * live).astype(BF16)
    own_up = lax.dynamic_slice_in_dim(up_rows, replica * block, block, 1)
    own_down = lax.dynamic_slice_in_dim(down_rows, replica * block, block, 1)
    act_known = jnp.concatenate([down_act, own_up], axis=1)
    act_all = [act_known] + [xor_permute(act_known, ("y", "c"), sections, j) for j in range(1, sections)]

    def cut(after):
        return run(cut_weight, [weight], [shape_of((block, wide))] * quarters, after=after)

    pieces = cut(act_all[1:])

    outs = run(
        first_rows,
        act_all + [cotangent, weight, up_rows, own_down],
        [
            shape_of((replicas, plan.group + rank, wide)),
            shape_of((replicas, (sections - 2) * plan.group, wide)),
        ],
        scratch=[
            pltpu.VMEM((sections, rank, tokens + block), BF16),
            pltpu.VMEM((nz, (sections - 1) * plan.group, part), BF16),
            pltpu.VMEM((rank, features), BF16),
        ],
        after=[pieces[1]],
    )
    lead = lax.all_to_all(outs[0], ("z", "x"), split_axis=0, concat_axis=0)

    def send_weight(pieces, core, step):
        pairs = []
        for y in range(ny):
            for x in range(nx):
                if y * nc + core > 0:
                    other = (y * nx + x) ^ step
                    pairs.append(
                        (((y * nc + core) * nx) + x, ((other // nx) * nc + core) * nx + other % nx)
                    )
        return lax.ppermute(pieces[step], ("y", "c", "x"), pairs)

    start = lax.dynamic_slice_in_dim(down_rows, iz * part, part, 1)
    adapters = jnp.concatenate([up_rows, start], axis=1)
    known = [adapters] + [xor_permute(adapters, ("y", "c"), sections, j) for j in range(1, sections)]
    up_quarter, up_part, down_part = run(
        sort_adapters,
        known,
        [shape_of((sections, rank, wide)), shape_of((sections, rank, part)), shape_of((sections, rank, part))],
        after=[outs[0]],
    )

    own, twin = {}, {}

    later = cut([outs[0]])

    def share(core, pieces, after):
        held = [pieces[0]] + [send_weight(pieces, core, step) for step in range(1, quarters)]
        (own[core],) = run(collect, held, [shape_of((quarters, block, wide))], after=after)
        twin[core] = lax.ppermute(own[core], "c", [(core, c) for c in range(nc) if c != core])

    share(nc - 1, pieces, [up_quarter, later[1]])

    def weight_specs(t):
        y = t // nc
        spec = pl.BlockSpec((nx, block, wide), lambda i: (y, 0, 0))
        return [spec, spec]

    finals = {}

    def stage(t, rows, after=()):
        count, height = len(rows), rows[0].shape[0]
        made = run(
            stage_rows,
            rows + [own[t % nc], twin[t % nc], up_quarter, down_part],
            [shape_of((height, width))] * quarters,
            scratch=[
                pltpu.VMEM((height if count > 1 else 8, wide), BF16),
                pltpu.VMEM((quarters, height, width), BF16),
            ],
            specs=[VMEM] * count + weight_specs(t) + [VMEM, VMEM],
            extra=(t, count),
            after=after,
        )
        total = made[0].astype(F32)
        for step in range(1, quarters):
            total = total + xor_permute(made[step], ("y", "x"), quarters, step).astype(F32)
        return total, made[0]

    def to_parts(keep):
        mine = keep.astype(BF16)
        return [mine] + [xor_permute(mine, "z", nz, m) for m in range(1, nz)]

    marks, sent = {}, {}
    rows = [lead[:, : plan.group].reshape(replicas * plan.group, wide)]
    for t in range(sections - 1, 0, -1):
        total, marks[t] = stage(t, rows)
        if t > 1:
            rows = to_parts(total)
            sent[t] = rows[0]
        if t == sections - 1:
            for core in range(nc - 2, -1, -1):
                share(core, later, [sent[t]])
    finals[0] = total
    rows = lax.all_to_all(outs[1], ("z", "x"), split_axis=0, concat_axis=0)
    rows = [rows.reshape(-1, wide)]
    for t in range(sections - 1, 1, -1):
        total, _ = stage(t, rows, [sent[t]])
        total = total.reshape(replicas, t - 1, plan.group, width)
        finals[t - 1] = total[:, -1]
        if t > 2:
            rows = to_parts(total[:, :-1].reshape(-1, width))

    seed = jnp.sum(lead[:, plan.group :].astype(F32), axis=0).astype(BF16)
    seed = lax.dynamic_slice_in_dim(seed, replica * block % LANES, block, 1)
    seed = jnp.where(ic == 1 % nc, seed, lax.ppermute(seed, "c", [(1 % nc, c) for c in range(nc) if c != 1 % nc]))
    seeds = [seed] + [xor_permute(seed, ("y", "x"), quarters, k) for k in range(1, quarters)]
    seeds = jnp.stack(seeds)
    home = (1 // nc) * nx
    prefix = [
        jnp.concatenate(
            [lax.dynamic_index_in_dim(seeds, quarter ^ (home + x), 0, keepdims=False) for x in range(nx)], axis=1
        )
    ]
    for t in range(2, sections):
        split = t < sections - 1
        count = len(prefix)
        height = t * rank
        made = run(
            carry_rows,
            prefix + [own[t % nc], twin[t % nc], up_quarter, up_part, down_part],
            [shape_of((height, width))] * nz if split else [shape_of((height, wide))],
            scratch=[pltpu.VMEM((height, width * quarters), BF16)],
            specs=[VMEM] * count + weight_specs(t) + [VMEM] * 3,
            extra=(t, count, split),
            after=[sent[sections + 1 - t]],
        )
        if split:
            total = made[0].astype(F32)
            for m in range(1, nz):
                total = total + xor_permute(made[m], "z", nz, m).astype(F32)
            total = total.astype(BF16)
            prefix = [total] + [xor_permute(total, ("y", "x"), quarters, k) for k in range(1, quarters)]
        else:
            total = made[0].astype(F32).reshape(height, nz, width)
            for m in range(1, nz):
                other = xor_permute(made[0], "z", nz, m).astype(F32)
                total = total + jnp.concatenate(
                    [other[:, (j ^ m) * width : ((j ^ m) + 1) * width] for j in range(nz)], axis=1
                ).reshape(height, nz, width)
            total = total.astype(BF16).reshape(sections - 1, rank, wide)
            picked = []
            for k in range(quarters):
                target = (quarter ^ k) // nx * nc + ic
                picked.append(
                    lax.dynamic_index_in_dim(total, jnp.minimum(target, sections - 2), 0, keepdims=False)
                )
            prefix = [picked[0]] + [
                xor_permute(picked[k], ("y", "x"), quarters, k) for k in range(1, quarters)
            ]

    down_terms, top_terms, own_squares = run(
        own_terms,
        prefix + [up_rows, cotangent, inputs, live, down_act],
        [shape_of((slots, rank, features), F32), shape_of((slots, rank, features), F32), shape_of((slots, LANES), F32)],
        scratch=[pltpu.VMEM((rank, features), BF16)],
        after=[marks[1]],
    )

    mine = (jnp.arange(replicas) == replica).astype(F32)[:, None] * own_squares[:, 0][None, :]
    carried = {s: finals[s].reshape(replicas, half, rank, width) for s in finals}
    squares = sum(jnp.sum(value * value, axis=(2, 3)) for value in carried.values())
    squares = (jnp.arange(nc) == ic).astype(F32)[None, :, None] * squares[:, None, :]
    squares = (mine + squares.reshape(replicas, slots)).reshape(1, 1, replicas * slots)
    squares = jnp.broadcast_to(squares, (sections * replicas, 8, replicas * slots))
    squares = lax.all_to_all(squares, ("y", "c", "z", "x"), split_axis=0, concat_axis=0)
    totals = jnp.sum(squares[:, 0], axis=0).reshape(replicas, slots)
    norms = jnp.sqrt(totals)
    factors = clip_scale / (norms + 0.01)

    own_norms = lax.dynamic_index_in_dim(norms, replica, 0, keepdims=False)
    own_factors = lax.dynamic_index_in_dim(factors, replica, 0, keepdims=False)[:, None, None]
    sums = jnp.stack([jnp.sum(own_factors * down_terms, axis=0), jnp.sum(own_factors * top_terms, axis=0)])
    sums = sums.astype(BF16).reshape(2 * rank, replicas, block).transpose(1, 0, 2)
    sums = lax.all_to_all(sums, ("z", "x"), split_axis=0, concat_axis=0)
    sums = jnp.sum(sums.astype(F32), axis=0)
    grad_down, top_up = sums[:rank], sums[rank:]

    core_factors = lax.dynamic_index_in_dim(factors.reshape(replicas, nc, half), ic, 1, keepdims=False)
    scaled = [jnp.sum(core_factors[:, :, None, None] * carried[s], axis=(0, 1)) for s in range(sections - 1)]
    scaled.append(jnp.zeros_like(scaled[0]))
    scaled = jnp.stack(scaled)
    place = section * nx + ix
    found = []
    for k in range(sections * nx):
        part_rows = lax.dynamic_index_in_dim(scaled, (place ^ k) // nx, 0, keepdims=False)
        found.append(part_rows if k == 0 else xor_permute(part_rows, ("y", "c", "x"), sections * nx, k))
    found = jnp.stack(found).reshape(ny, nc, nx, rank, width)
    found = jnp.sum(found, axis=1).reshape(quarters, rank, width)
    scaled = jnp.concatenate(
        [lax.dynamic_index_in_dim(found, quarter ^ q, 0, keepdims=False) for q in range(quarters)], axis=1
    )
    low_up = lax.dynamic_slice_in_dim(scaled, ix * block, block, 1)
    grad_up = jnp.where(last, top_up, low_up)
    example_norms = jnp.sum(choose.astype(F32) * own_norms[:, None], axis=0)
    return (grad_down[None], grad_up[None], example_norms[None])


def solution(mesh):
    sections, replicas = mesh.shape["section"], mesh.shape["dp"]
    nc = 2
    ny = sections // nc
    nx = ny
    nz = replicas // nx
    fine = Mesh(mesh.devices.reshape(ny, nc, nz, nx), ("y", "c", "z", "x"))
    section, dp = ("y", "c"), ("z", "x")
    in_specs = (
        P(section, dp, None),
        P(dp, None),
        P(section, dp, None),
        P(section, None, None),
        P(section, None, None),
        P(dp, None),
        P(dp, None),
    )
    out_specs = (P(section, None, dp), P(section, None, dp), P(dp, None))

    return jax.shard_map(on_device, mesh=fine, in_specs=in_specs, out_specs=out_specs, check_vma=False)
```

time: 878 us -> 268 us (0.31)
  waiting for transfers between devices: 723 us -> 67.9 us
  starting transfers between devices: 9.08 us -> 105 us
  matrix products: 74.9 us -> 3.08 us
  Pallas kernels: 0 us -> 62.2 us
  blocking collectives: 12.7 us -> 0 us
  between operations: 13.9 us -> 1.63 us
  other arithmetic: 21.9 us -> 10.2 us
    all_gather x1 -> x0, waiting for transfers between devices: 488 us -> none  [on_device(): weight = lax.all_gather(frozen[0], 'dp', axis=0, tiled=True)]
    unnamed x5 -> x0, waiting for transfers between devices: 131 us -> none
    ppermute x7 -> x61, starting transfers between devices: 8.96 us -> 85 us  [the longest x52 73.1 us: xor_permute(): return lax.ppermute(value, axes, [(i, i ^ step) for i in range(count)])]
    dot_general x16 -> x1, matrix products: 74.9 us -> 3.08 us  [mm(): lax.dot_general(left, right, (dims, ((), ())), preferred_element_type=F32)]
    ppermute x7 -> x61, waiting for transfers between devices: 104 us -> 38.6 us  [the longest x52 36.8 us: xor_permute(): return lax.ppermute(value, axes, [(i, i ^ step) for i in range(count)])]
    pallas_call x0 -> x14, Pallas kernels: none -> 62.2 us  [local_call(): pl.pallas_call(body, out_shape=shapes, grid=(1,), in_specs=[SMEM] + specs...]
    all_to_all x0 -> x4, waiting for transfers between devices: none -> 29.4 us  [the longest x1 15.9 us: on_device(): lead = lax.all_to_all(outs[0], ('z', 'x'), split_axis=0, concat_axis=0)]
    all_to_all x0 -> x4, starting transfers between devices: none -> 20 us  [the longest x1 7.15 us: on_device(): rows = lax.all_to_all(outs[1], ('z', 'x'), split_axis=0, concat_axis=0)]
  transfers between devices with their start and end apart: 10 -> 65, of which waited for: 10 -> 19; matrix products, arithmetic and copies ran while one was open for 2% -> 5% of each run, Pallas kernels for 0% -> 18%
where the time goes in v1:
time: 268 us; the launch traced here: 267 us
  starting transfers between devices  105 us (39%)
  waiting for transfers between devices  67.9 us (25%)
  Pallas kernels  62.2 us (23%)
  local copies, waits for them, and re-layouts  16.8 us (6%)
  other arithmetic  10.2 us (4%)
  matrix products  3.08 us (1%)
    ppermute x52, starting transfers between devices, xor_permute(): return lax.ppermute(value, axes, [(i, i ^ step) for i in range(count)])  73.1 us
    pallas_call x14, Pallas kernels, local_call(): pl.pallas_call(body, out_shape=shapes, grid=(1,), in_specs=[SMEM] + specs...  62.2 us
    ppermute x52, waiting for transfers between devices, xor_permute(): return lax.ppermute(value, axes, [(i, i ^ step) for i in range(count)])  36.8 us
    all_to_all x1, waiting for transfers between devices, on_device(): lead = lax.all_to_all(outs[0], ('z', 'x'), split_axis=0, concat_axis=0)  15.9 us
    unnamed x104, local copies, waits for them, and re-layouts  9.04 us
    all_to_all x1, starting transfers between devices, on_device(): rows = lax.all_to_all(outs[1], ('z', 'x'), split_axis=0, concat_axis=0)  7.15 us
    all_to_all x1, waiting for transfers between devices, on_device(): lax.all_to_all(squares, ('y', 'c', 'z', 'x'), split_axis=0, concat_axis=0)  6.89 us
    all_to_all x1, waiting for transfers between devices, on_device(): rows = lax.all_to_all(outs[1], ('z', 'x'), split_axis=0, concat_axis=0)  6.62 us
  transfers between devices with their start and end apart: 65, of which 19 were waited for; matrix products, arithmetic and copies ran while one was open for 5% of the time, Pallas kernels for 18%

profile of v1, /device:TPU:0, one launch (start us, length us, event | category | flops | bytes accessed | tf_op | source)
XLA Modules:
  0.0 267.0 jit_solution(3477182257737700679)
XLA Ops:
  3.1 3.1 %fusion.2.refs_9_ = bf16[16,512]{1,0:T(8,128)(2,1)S(1)} fusion(bf16[1,16,3584]{2,1,0:T(8,128)(2,1)S(1)} %copy-done, f32[512]{0:T(512)S(1)} %get-tuple-element.124, bf16[1,512,3584]{2,1,0:T(8,128)(2,1)} %param.7), kind=kOutput, calls=%fused_computation.3 | convolution fusion | flops 58753024 | bytes 3803136 | tf_op jit(solution)/shard_map/dot_general | solution.py:18
  6.2 2.5 collective-permute-start.2
  13.3 4.8 %shard_map.94 = (bf16[448,1024]{1,0:T(8,128)(2,1)}, bf16[448,1024]{1,0:T(8,128)(2,1)}, bf16[448,1024]{1,0:T(8,128)(2,1)}, bf16[448,1024]{1,0:T(8,128)(2,1)}) custom-call(s32[7]{0:T(128)} %stack.95.at, bf16[16,960]{1,0:T(8,128)(2,1)} %copy-done.33, bf16[16,960]{1,0:T(8,128)(2,1)} %copy-done.32, bf16[16,960]{1,0:T(8,128)(2,1)} %copy-done.31, ...), custom_call_target="tpu_custom_call" | custom-call | tf_op jit(solution)/shard_map/pallas_call | solution.py:31
  20.3 7.0 %collective-permute-start.5 = (bf16[16,4480]{1,0:T(8,128)(2,1)S(1)}, bf16[16,4480]{1,0:T(8,128)(2,1)S(1)}, u32[]{:S(2)}, u32[]{:S(2)}) collective-permute-start(bf16[16,4480]{1,0:T(8,128)(2,1)S(1)} %pad_maximum_fusion.1.refs_1_), channel_id=1, source_target_pairs={{0,24},{8,16},{16,8},{24,0},{1,25},{9,17},{17,9},{25,1},{2,26},{10... | collective-permute-start | bytes 430088 | tf_op jit(solution)/shard_map/ppermute | solution.py:47
  28.1 18.8 %collective-permute-done.5.refs_4_ = bf16[16,4480]{1,0:T(8,128)(2,1)S(1)} collective-permute-done((bf16[16,4480]{1,0:T(8,128)(2,1)S(1)}, bf16[16,4480]{1,0:T(8,128)(2,1)S(1)}, u32[]{:S(2)}, u32[]{:S(2)}) %collective-permute-start.5) | collective-permute-done | bytes 143392 | tf_op jit(solution)/shard_map/ppermute | solution.py:47
  47.6 5.2 %shard_map.95 = (bf16[8,48,1024]{2,1,0:T(8,128)(2,1)}, bf16[8,64,1024]{2,1,0:T(8,128)(2,1)}) custom-call(s32[7]{0:T(128)} %stack.95.at, bf16[448,1024]{1,0:T(8,128)(2,1)} %get-tuple-element.43.refs_0_, bf16[16,960]{1,0:T(8,128)(2,1)} %copy-done.34, bf16[16,960]{1,0:T(8,128)(2,1)} %copy-done.33, bf16[16,960]{1,0:T(8,128)(2,1)} %copy-done.32, ...), custom_call_target="tpu_custom_call" | custom-call | tf_op jit(solution)/shard_map/pallas_call | solution.py:31
  52.7 4.8 %shard_map.97 = (bf16[448,1024]{1,0:T(8,128)(2,1)}, bf16[448,1024]{1,0:T(8,128)(2,1)}, bf16[448,1024]{1,0:T(8,128)(2,1)}, bf16[448,1024]{1,0:T(8,128)(2,1)}) custom-call(s32[7]{0:T(128)} %stack.95.at, bf16[8,48,1024]{2,1,0:T(8,128)(2,1)} %get-tuple-element.44.refs_0_, bf16[448,3584]{1,0:T(8,128)(2,1)} %bitcast.112), custom_call_target="tpu_custom_call" | custom-call | tf_op jit(solution)/shard_map/pallas_call | solution.py:31
  62.3 4.2 %shard_map.98.refs_1_.refs_4_.refs_5_.refs_2_ = bf16[4,448,1024]{2,1,0:T(8,128)(2,1)} custom-call(s32[7]{0:T(128)} %stack.95.at, bf16[4,16,1024]{2,1,0:T(8,128)(2,1)} %get-tuple-element.45.refs_0_.refs_3_.refs_6_.refs_4_.refs_7_, bf16[448,1024]{1,0:T(8,128)(2,1)} %get-tuple-element.46.refs_1_, bf16[448,1024]{1,0:T(8,128)(2,1)} %get-tuple-element.47.refs_2_, ...), custom_call_target="tpu_custom_call" | custom-call | tf_op jit(solution)/shard_map/pallas_call | solution.py:31
  67.7 5.8 %all-to-all-start = ((bf16[8,48,1024]{2,1,0:T(8,128)(2,1)}), bf16[8,48,1024]{2,1,0:T(8,128)(2,1)S(1)}, u32[]{:S(2)}, u32[]{:S(2)}) async-start(bf16[8,48,1024]{2,1,0:T(8,128)(2,1)} %get-tuple-element.44.refs_0_), calls=%async_computation | async-start | bytes 1572864 | tf_op jit(solution)/shard_map/all_to_all | solution.py:309
  77.8 15.9 %all-to-all-done = bf16[8,48,1024]{2,1,0:T(8,128)(2,1)S(1)} async-done(((bf16[8,48,1024]{2,1,0:T(8,128)(2,1)}), bf16[8,48,1024]{2,1,0:T(8,128)(2,1)S(1)}, u32[]{:S(2)}, u32[]{:S(2)}) %all-to-all-start) | async-done | bytes 786464 | tf_op jit(solution)/shard_map/all_to_all | solution.py:309
  94.5 4.4 %shard_map.99 = (bf16[256,256]{1,0:T(8,128)(2,1)}, bf16[256,256]{1,0:T(8,128)(2,1)}, bf16[256,256]{1,0:T(8,128)(2,1)}, bf16[256,256]{1,0:T(8,128)(2,1)}) custom-call(s32[7]{0:T(128)} %stack.95.at, bf16[256,1024]{1,0:T(8,128)(2,1)} %bitcast.118, bf16[4,448,1024]{2,1,0:T(8,128)(2,1)} %shard_map.98.refs_1_.refs_4_.refs_5_.refs_2_, ...), custom_call_target="tpu_custom_call" | custom-call | tf_op jit(solution)/shard_map/pallas_call | solution.py:31
  102.0 2.7 %collective-permute-done.10 = bf16[256,256]{1,0:T(8,128)(2,1)S(1)} collective-permute-done((bf16[256,256]{1,0:T(8,128)(2,1)}, bf16[256,256]{1,0:T(8,128)(2,1)S(1)}, u32[]{:S(2)}, u32[]{:S(2)}) %collective-permute-start.10) | collective-permute-done | bytes 131104 | tf_op jit(solution)/shard_map/ppermute | solution.py:47
  104.7 5.1 %collective-permute-start.12 = (bf16[256,256]{1,0:T(8,128)(2,1)}, bf16[256,256]{1,0:T(8,128)(2,1)S(1)}, u32[]{:S(2)}, u32[]{:S(2)}) collective-permute-start(bf16[256,256]{1,0:T(8,128)(2,1)} %get-tuple-element.54), channel_id=1, source_target_pairs={{0,17},{1,16},{16,1},{17,0},{2,19},{3,18},{18,3},{19,2},{4,21},{5,... | collective-permute-start | bytes 393224 | tf_op jit(solution)/shard_map/ppermute | solution.py:47
  109.8 3.2 %collective-permute-done.12 = bf16[256,256]{1,0:T(8,128)(2,1)S(1)} collective-permute-done((bf16[256,256]{1,0:T(8,128)(2,1)}, bf16[256,256]{1,0:T(8,128)(2,1)S(1)}, u32[]{:S(2)}, u32[]{:S(2)}) %collective-permute-start.12) | collective-permute-done | bytes 131104 | tf_op jit(solution)/shard_map/ppermute | solution.py:47
  115.5 4.2 %shard_map.100.refs_4_.refs_2_.refs_5_ = bf16[4,448,1024]{2,1,0:T(8,128)(2,1)} custom-call(s32[7]{0:T(128)} %stack.95.at, bf16[256,256]{1,0:T(8,128)(2,1)} %add_convert_fusion.1.refs_0_, bf16[448,1024]{1,0:T(8,128)(2,1)} %get-tuple-element.55.refs_1_, bf16[448,1024]{1,0:T(8,128)(2,1)} %collective-permute-done.16.refs_2_, bf16[448,1024]{1,0:T(8,128)(2,1)} %copy-done.12, ...), custom_call_target="tpu_custom_call" | custom-call | tf_op jit(solution)/shard_map/pallas_call | solution.py:31
  119.7 3.1 %collective-permute-start.19 = (bf16[4,448,1024]{2,1,0:T(8,128)(2,1)}, bf16[4,448,1024]{2,1,0:T(8,128)(2,1)}, u32[]{:S(2)}, u32[]{:S(2)}) collective-permute-start(bf16[4,448,1024]{2,1,0:T(8,128)(2,1)} %shard_map.100.refs_4_.refs_2_.refs_5_), channel_id=1, source_target_pairs={{0,8},{1,9},{2,10},{3,11},{4,12},{5,13},{6,14},{7,15},{16,24},{17,... | collective-permute-start | bytes 11010056 | tf_op jit(solution)/shard_map/ppermute | solution.py:339
  122.8 7.2 %all-to-all-start.1 = ((bf16[8,64,1024]{2,1,0:T(8,128)(2,1)}), bf16[8,64,1024]{2,1,0:T(8,128)(2,1)S(1)}, u32[]{:S(2)}, u32[]{:S(2)}) async-start(bf16[8,64,1024]{2,1,0:T(8,128)(2,1)} %get-tuple-element.72), calls=%async_computation.1 | async-start | bytes 2097152 | tf_op jit(solution)/shard_map/all_to_all | solution.py:384
  133.2 3.5 %collective-permute-start.29 = (bf16[16,448]{1,0:T(8,128)(2,1)S(1)}, bf16[16,448]{1,0:T(8,128)(2,1)S(1)}, u32[]{:S(2)}, u32[]{:S(2)}) collective-permute-start(bf16[16,448]{1,0:T(8,128)(2,1)S(1)} %broadcast_select_fusion), channel_id=1, source_target_pairs={{0,17},{1,16},{16,1},{17,0},{2,19},{3,18},{18,3},{19,2},{4,21},{5,... | collective-permute-start | bytes 43016 | tf_op jit(solution)/shard_map/ppermute | solution.py:47
  137.3 2.3 collective-permute-done.29
  140.5 4.3 %collective-permute-start.15 = (bf16[256,256]{1,0:T(8,128)(2,1)S(1)}, bf16[256,256]{1,0:T(8,128)(2,1)S(1)}, u32[]{:S(2)}, u32[]{:S(2)}) collective-permute-start(bf16[256,256]{1,0:T(8,128)(2,1)S(1)} %copy-done.2), channel_id=1, source_target_pairs={{0,6},{2,4},{4,2},{6,0},{1,7},{3,5},{5,3},{7,1},{8,14},{10,12},{12... | collective-permute-start | bytes 393224 | tf_op jit(solution)/shard_map/ppermute | solution.py:47
  146.2 3.3 %shard_map.103 = (bf16[32,256]{1,0:T(8,128)(2,1)}, bf16[32,256]{1,0:T(8,128)(2,1)}, bf16[32,256]{1,0:T(8,128)(2,1)}, bf16[32,256]{1,0:T(8,128)(2,1)}) custom-call(s32[7]{0:T(128)} %stack.95.at, bf16[256,256]{1,0:T(8,128)(2,1)} %add_convert_fusion.1.refs_0_, bf16[16,896]{1,0:T(8,128)(2,1)} %pad_maximum_fusion.4.refs_1_, ...), custom_call_target="tpu_custom_call" | custom-call | tf_op jit(solution)/shard_map/pallas_call | solution.py:31
  150.8 6.6 %all-to-all-done.1 = bf16[8,64,1024]{2,1,0:T(8,128)(2,1)S(1)} async-done(((bf16[8,64,1024]{2,1,0:T(8,128)(2,1)}), bf16[8,64,1024]{2,1,0:T(8,128)(2,1)S(1)}, u32[]{:S(2)}, u32[]{:S(2)}) %all-to-all-start.1) | async-done | bytes 1048608 | tf_op jit(solution)/shard_map/all_to_all | solution.py:384
  158.5 6.0 %shard_map.106 = (bf16[512,256]{1,0:T(8,128)(2,1)}, bf16[512,256]{1,0:T(8,128)(2,1)}, bf16[512,256]{1,0:T(8,128)(2,1)}, bf16[512,256]{1,0:T(8,128)(2,1)}) custom-call(s32[7]{0:T(128)} %stack.95.at, bf16[256,256]{1,0:T(8,128)(2,1)} %add_convert_fusion.1.refs_0_, bf16[512,1024]{1,0:T(8,128)(2,1)} %bitcast.114, ...), custom_call_target="tpu_custom_call" | custom-call | tf_op jit(solution)/shard_map/pallas_call | solution.py:31
  170.1 4.6 %shard_map.101 = (bf16[256,256]{1,0:T(8,128)(2,1)}, bf16[256,256]{1,0:T(8,128)(2,1)}, bf16[256,256]{1,0:T(8,128)(2,1)}, bf16[256,256]{1,0:T(8,128)(2,1)}) custom-call(s32[7]{0:T(128)} %stack.95.at, bf16[256,256]{1,0:T(8,128)(2,1)} %add_convert_fusion.1.refs_0_, bf16[256,256]{1,0:T(8,128)(2,1)} %copy-done.24, bf16[256,256]{1,0:T(8,128)(2,1)} %copy-done.23, ...), custom_call_target="tpu_custom_call" | custom-call | tf_op jit(solution)/shard_map/pallas_call | solution.py:31
  180.3 2.4 collective-permute-start.50
  191.6 3.4 %shard_map.104 = bf16[48,1024]{1,0:T(8,128)(2,1)} custom-call(s32[7]{0:T(128)} %stack.95.at, bf16[256,256]{1,0:T(8,128)(2,1)} %add_convert_fusion.refs_0_, bf16[32,256]{1,0:T(8,128)(2,1)} %copy-done.35, bf16[32,256]{1,0:T(8,128)(2,1)} %copy-done.41, bf16[32,256]{1,0:T(8,128)(2,1)} %copy-done.40, bf16[32,256]{1,0:T(8,128)(2,1)} %copy-done.39, ...), custom_call_target="tpu_custom_call" | custom-call | tf_op jit(solution)/shard_map/pallas_call | solution.py:31
  202.3 4.4 %shard_map.107 = (bf16[256,256]{1,0:T(8,128)(2,1)}, bf16[256,256]{1,0:T(8,128)(2,1)}, bf16[256,256]{1,0:T(8,128)(2,1)}, bf16[256,256]{1,0:T(8,128)(2,1)}) custom-call(s32[7]{0:T(128)} %stack.95.at, bf16[256,256]{1,0:T(8,128)(2,1)} %add_convert_fusion.refs_0_, bf16[256,256]{1,0:T(8,128)(2,1)} %bitcast.129, bf16[256,256]{1,0:T(8,128)(2,1)} %copy-done.29, ...), custom_call_target="tpu_custom_call" | custom-call | tf_op jit(solution)/shard_map/pallas_call | solution.py:31
  219.7 4.4 %shard_map.102 = (bf16[256,256]{1,0:T(8,128)(2,1)}, bf16[256,256]{1,0:T(8,128)(2,1)}, bf16[256,256]{1,0:T(8,128)(2,1)}, bf16[256,256]{1,0:T(8,128)(2,1)}) custom-call(s32[7]{0:T(128)} %stack.95.at, bf16[256,256]{1,0:T(8,128)(2,1)} %add_convert_fusion.refs_0_, bf16[256,256]{1,0:T(8,128)(2,1)} %copy-done.30, bf16[256,256]{1,0:T(8,128)(2,1)} %copy-done.26, ...), custom_call_target="tpu_custom_call" | custom-call | tf_op jit(solution)/shard_map/pallas_call | solution.py:31
  228.3 6.7 %shard_map.105 = (f32[4,16,3584]{2,1,0:T(8,128)}, f32[4,16,3584]{2,1,0:T(8,128)}, f32[4,128]{1,0:T(4,128)}) custom-call(s32[7]{0:T(128)} %stack.95.at, bf16[256,256]{1,0:T(8,128)(2,1)} %get-tuple-element.62.refs_0_, bf16[16,1024]{1,0:T(8,128)(2,1)} %get-tuple-element.94.refs_1_, bf16[16,1024]{1,0:T(8,128)(2,1)} %copy-done.38, bf16[16,1024]{1,0:T(8,128)(2,1)} %copy-done.37, ...), custom_call_target="tpu_custom_call" | custom-call | tf_op jit(solution)/shard_map/pallas_call | solution.py:31
  237.5 3.7 %all-to-all-start.2 = ((f32[32,1,256]{2,1,0:T(1,128)}), f32[32,1,256]{2,1,0:T(1,128)S(1)}, u32[]{:S(2)}, u32[]{:S(2)}) async-start(f32[32,1,256]{2,1,0:T(1,128)} %reshape.159), calls=%async_computation.2 | async-start | bytes 65536 | tf_op jit(solution)/shard_map/all_to_all | solution.py:455
  241.4 6.9 %all-to-all-done.2 = f32[32,1,256]{2,1,0:T(1,128)S(1)} async-done(((f32[32,1,256]{2,1,0:T(1,128)}), f32[32,1,256]{2,1,0:T(1,128)S(1)}, u32[]{:S(2)}, u32[]{:S(2)}) %all-to-all-start.2) | async-done | bytes 32800 | tf_op jit(solution)/shard_map/all_to_all | solution.py:455
  253.3 3.4 %all-to-all-start.3 = ((bf16[8,32,448]{2,1,0:T(8,128)(2,1)}), bf16[8,32,448]{2,1,0:T(8,128)(2,1)S(1)}, u32[]{:S(2)}, u32[]{:S(2)}) async-start(bf16[8,32,448]{2,1,0:T(8,128)(2,1)} %copy.48), calls=%async_computation.3 | async-start | bytes 524288 | tf_op jit(solution)/shard_map/all_to_all | solution.py:464
  (296 shorter events, 97.8 us)
Async XLA Ops:
  18.1 42.7 %collective-permute-start.7 = (bf16[448,1024]{1,0:T(8,128)(2,1)}, bf16[448,1024]{1,0:T(8,128)(2,1)S(1)}, u32[]{:S(2)}, u32[]{:S(2)}) collective-permute-start(bf16[448,1024]{1,0:T(8,128)(2,1)} %get-tuple-element.48), channel_id=1, source_target_pairs={{8,24},{9,25},{24,8},{25,9},{10,26},{11,27},{26,10},{27,11},{12,28... | collective-permute-start | bytes 2752520 | tf_op jit(solution)/shard_map/ppermute | solution.py:320
  18.8 42.0 %collective-permute-start.8 = (bf16[448,1024]{1,0:T(8,128)(2,1)}, bf16[448,1024]{1,0:T(8,128)(2,1)S(1)}, u32[]{:S(2)}, u32[]{:S(2)}) collective-permute-start(bf16[448,1024]{1,0:T(8,128)(2,1)} %get-tuple-element.49), channel_id=1, source_target_pairs={{8,25},{9,24},{24,9},{25,8},{10,27},{11,26},{26,11},{27,10},{12,29... | collective-permute-start | bytes 2752520 | tf_op jit(solution)/shard_map/ppermute | solution.py:320
  19.5 41.3 %collective-permute-start.6 = (bf16[448,1024]{1,0:T(8,128)(2,1)}, bf16[448,1024]{1,0:T(8,128)(2,1)S(1)}, u32[]{:S(2)}, u32[]{:S(2)}) collective-permute-start(bf16[448,1024]{1,0:T(8,128)(2,1)} %get-tuple-element.43.refs_0_), channel_id=1, source_target_pairs={{8,9},{9,8},{24,25},{25,24},{10,11},{11,10},{26,27},{27,26},{12,13... | collective-permute-start | bytes 2752520 | tf_op jit(solution)/shard_map/ppermute | solution.py:320
  20.3 26.5 %collective-permute-start.5 = (bf16[16,4480]{1,0:T(8,128)(2,1)S(1)}, bf16[16,4480]{1,0:T(8,128)(2,1)S(1)}, u32[]{:S(2)}, u32[]{:S(2)}) collective-permute-start(bf16[16,4480]{1,0:T(8,128)(2,1)S(1)} %pad_maximum_fusion.1.refs_1_), channel_id=1, source_target_pairs={{0,24},{8,16},{16,8},{24,0},{1,25},{9,17},{17,9},{25,1},{2,26},{10... | collective-permute-start | bytes 430088 | tf_op jit(solution)/shard_map/ppermute | solution.py:47
  27.3 30.2 %collective-permute-start.4 = (bf16[16,4480]{1,0:T(8,128)(2,1)S(1)}, bf16[16,4480]{1,0:T(8,128)(2,1)S(1)}, u32[]{:S(2)}, u32[]{:S(2)}) collective-permute-start(bf16[16,4480]{1,0:T(8,128)(2,1)S(1)} %pad_maximum_fusion.1.refs_1_), channel_id=1, source_target_pairs={{0,16},{8,24},{16,0},{24,8},{1,17},{9,25},{17,1},{25,9},{2,18},{10... | collective-permute-start | bytes 430088 | tf_op jit(solution)/shard_map/ppermute | solution.py:47
  66.5 28.0 %collective-permute-start.9 = (bf16[4,448,1024]{2,1,0:T(8,128)(2,1)}, bf16[4,448,1024]{2,1,0:T(8,128)(2,1)}, u32[]{:S(2)}, u32[]{:S(2)}) collective-permute-start(bf16[4,448,1024]{2,1,0:T(8,128)(2,1)} %shard_map.98.refs_1_.refs_4_.refs_5_.refs_2_), channel_id=1, source_target_pairs={{8,0},{9,1},{10,2},{11,3},{12,4},{13,5},{14,6},{15,7},{24,16},{25,... | collective-permute-start | bytes 11010056 | tf_op jit(solution)/shard_map/ppermute | solution.py:339
  67.7 25.9 %all-to-all-start = ((bf16[8,48,1024]{2,1,0:T(8,128)(2,1)}), bf16[8,48,1024]{2,1,0:T(8,128)(2,1)S(1)}, u32[]{:S(2)}, u32[]{:S(2)}) async-start(bf16[8,48,1024]{2,1,0:T(8,128)(2,1)} %get-tuple-element.44.refs_0_), calls=%async_computation | async-start | bytes 1572864 | tf_op jit(solution)/shard_map/all_to_all | solution.py:309
  73.5 41.0 %collective-permute-start.17 = (bf16[448,1024]{1,0:T(8,128)(2,1)}, bf16[448,1024]{1,0:T(8,128)(2,1)S(1)}, u32[]{:S(2)}, u32[]{:S(2)}) collective-permute-start(bf16[448,1024]{1,0:T(8,128)(2,1)} %get-tuple-element.56), channel_id=1, source_target_pairs={{16,0},{17,1},{18,2},{19,3},{20,4},{21,5},{22,6},{23,7}} | collective-permute-start | bytes 2752520 | tf_op jit(solution)/shard_map/ppermute | solution.py:320
  74.8 39.7 %collective-permute-start.18 = (bf16[448,1024]{1,0:T(8,128)(2,1)}, bf16[448,1024]{1,0:T(8,128)(2,1)}, u32[]{:S(2)}, u32[]{:S(2)}) collective-permute-start(bf16[448,1024]{1,0:T(8,128)(2,1)} %get-tuple-element.57), channel_id=1, source_target_pairs={{16,1},{17,0},{18,3},{19,2},{20,5},{21,4},{22,7},{23,6}} | collective-permute-start | bytes 2752520 | tf_op jit(solution)/shard_map/ppermute | solution.py:320
  76.1 38.4 %collective-permute-start.16 = (bf16[448,1024]{1,0:T(8,128)(2,1)S(1)}, bf16[448,1024]{1,0:T(8,128)(2,1)}, u32[]{:S(2)}, u32[]{:S(2)}) collective-permute-start(bf16[448,1024]{1,0:T(8,128)(2,1)S(1)} %copy-done.6), channel_id=1, source_target_pairs={{16,17},{17,16},{18,19},{19,18},{20,21},{21,20},{22,23},{23,22}} | collective-permute-start | bytes 2752520 | tf_op jit(solution)/shard_map/ppermute | solution.py:320
  119.7 26.4 %collective-permute-start.19 = (bf16[4,448,1024]{2,1,0:T(8,128)(2,1)}, bf16[4,448,1024]{2,1,0:T(8,128)(2,1)}, u32[]{:S(2)}, u32[]{:S(2)}) collective-permute-start(bf16[4,448,1024]{2,1,0:T(8,128)(2,1)} %shard_map.100.refs_4_.refs_2_.refs_5_), channel_id=1, source_target_pairs={{0,8},{1,9},{2,10},{3,11},{4,12},{5,13},{6,14},{7,15},{16,24},{17,... | collective-permute-start | bytes 11010056 | tf_op jit(solution)/shard_map/ppermute | solution.py:339
  122.8 34.7 %all-to-all-start.1 = ((bf16[8,64,1024]{2,1,0:T(8,128)(2,1)}), bf16[8,64,1024]{2,1,0:T(8,128)(2,1)S(1)}, u32[]{:S(2)}, u32[]{:S(2)}) async-start(bf16[8,64,1024]{2,1,0:T(8,128)(2,1)} %get-tuple-element.72), calls=%async_computation.1 | async-start | bytes 2097152 | tf_op jit(solution)/shard_map/all_to_all | solution.py:384
  140.5 25.1 %collective-permute-start.15 = (bf16[256,256]{1,0:T(8,128)(2,1)S(1)}, bf16[256,256]{1,0:T(8,128)(2,1)S(1)}, u32[]{:S(2)}, u32[]{:S(2)}) collective-permute-start(bf16[256,256]{1,0:T(8,128)(2,1)S(1)} %copy-done.2), channel_id=1, source_target_pairs={{0,6},{2,4},{4,2},{6,0},{1,7},{3,5},{5,3},{7,1},{8,14},{10,12},{12... | collective-permute-start | bytes 393224 | tf_op jit(solution)/shard_map/ppermute | solution.py:47
  144.8 22.1 %collective-permute-start.14 = (bf16[256,256]{1,0:T(8,128)(2,1)S(1)}, bf16[256,256]{1,0:T(8,128)(2,1)S(1)}, u32[]{:S(2)}, u32[]{:S(2)}) collective-permute-start(bf16[256,256]{1,0:T(8,128)(2,1)S(1)} %copy-done.2), channel_id=1, source_target_pairs={{0,4},{2,6},{4,0},{6,2},{1,5},{3,7},{5,1},{7,3},{8,12},{10,14},{12... | collective-permute-start | bytes 393224 | tf_op jit(solution)/shard_map/ppermute | solution.py:47
  144.8 23.1 %collective-permute-start.13 = (bf16[256,256]{1,0:T(8,128)(2,1)S(1)}, bf16[256,256]{1,0:T(8,128)(2,1)S(1)}, u32[]{:S(2)}, u32[]{:S(2)}) collective-permute-start(bf16[256,256]{1,0:T(8,128)(2,1)S(1)} %copy-done.2), channel_id=1, source_target_pairs={{0,2},{2,0},{4,6},{6,4},{1,3},{3,1},{5,7},{7,5},{8,10},{10,8},{12,... | collective-permute-start | bytes 393224 | tf_op jit(solution)/shard_map/ppermute | solution.py:47
  149.4 18.6 %collective-permute-start.30 = (bf16[32,256]{1,0:T(8,128)(2,1)}, bf16[32,256]{1,0:T(8,128)(2,1)S(1)}, u32[]{:S(2)}, u32[]{:S(2)}) collective-permute-start(bf16[32,256]{1,0:T(8,128)(2,1)} %get-tuple-element.65), channel_id=1, source_target_pairs={{0,2},{2,0},{4,6},{6,4},{1,3},{3,1},{5,7},{7,5},{8,10},{10,8},{12,... | collective-permute-start | bytes 49160 | tf_op jit(solution)/shard_map/ppermute | solution.py:47
  164.4 12.7 %collective-permute-start.45 = (bf16[512,256]{1,0:T(8,128)(2,1)}, bf16[512,256]{1,0:T(8,128)(2,1)S(1)}, u32[]{:S(2)}, u32[]{:S(2)}) collective-permute-start(bf16[512,256]{1,0:T(8,128)(2,1)} %get-tuple-element.74), channel_id=1, source_target_pairs={{0,1},{1,0},{16,17},{17,16},{2,3},{3,2},{18,19},{19,18},{4,5},{5,4... | collective-permute-start | bytes 786440 | tf_op jit(solution)/shard_map/ppermute | solution.py:47
  165.6 12.8 %collective-permute-start.46 = (bf16[512,256]{1,0:T(8,128)(2,1)}, bf16[512,256]{1,0:T(8,128)(2,1)S(1)}, u32[]{:S(2)}, u32[]{:S(2)}) collective-permute-start(bf16[512,256]{1,0:T(8,128)(2,1)} %get-tuple-element.75), channel_id=1, source_target_pairs={{0,16},{1,17},{16,0},{17,1},{2,18},{3,19},{18,2},{19,3},{4,20},{5,... | collective-permute-start | bytes 786440 | tf_op jit(solution)/shard_map/ppermute | solution.py:47
  167.0 13.2 %collective-permute-start.47 = (bf16[512,256]{1,0:T(8,128)(2,1)}, bf16[512,256]{1,0:T(8,128)(2,1)S(1)}, u32[]{:S(2)}, u32[]{:S(2)}) collective-permute-start(bf16[512,256]{1,0:T(8,128)(2,1)} %get-tuple-element.76), channel_id=1, source_target_pairs={{0,17},{1,16},{16,1},{17,0},{2,19},{3,18},{18,3},{19,2},{4,21},{5,... | collective-permute-start | bytes 786440 | tf_op jit(solution)/shard_map/ppermute | solution.py:47
  180.3 18.4 %collective-permute-start.50 = (bf16[256,256]{1,0:T(8,128)(2,1)S(1)}, bf16[256,256]{1,0:T(8,128)(2,1)S(1)}, u32[]{:S(2)}, u32[]{:S(2)}) collective-permute-start(bf16[256,256]{1,0:T(8,128)(2,1)S(1)} %bitcast.126), channel_id=1, source_target_pairs={{0,6},{2,4},{4,2},{6,0},{1,7},{3,5},{5,3},{7,1},{8,14},{10,12},{12... | collective-permute-start | bytes 393224 | tf_op jit(solution)/shard_map/ppermute | solution.py:47
  183.6 15.2 %collective-permute-start.49 = (bf16[256,256]{1,0:T(8,128)(2,1)S(1)}, bf16[256,256]{1,0:T(8,128)(2,1)S(1)}, u32[]{:S(2)}, u32[]{:S(2)}) collective-permute-start(bf16[256,256]{1,0:T(8,128)(2,1)S(1)} %bitcast.127), channel_id=1, source_target_pairs={{0,4},{2,6},{4,0},{6,2},{1,5},{3,7},{5,1},{7,3},{8,12},{10,14},{12... | collective-permute-start | bytes 393224 | tf_op jit(solution)/shard_map/ppermute | solution.py:47
  185.4 15.6 %collective-permute-start.48 = (bf16[256,256]{1,0:T(8,128)(2,1)S(1)}, bf16[256,256]{1,0:T(8,128)(2,1)S(1)}, u32[]{:S(2)}, u32[]{:S(2)}) collective-permute-start(bf16[256,256]{1,0:T(8,128)(2,1)S(1)} %bitcast.128), channel_id=1, source_target_pairs={{0,2},{2,0},{4,6},{6,4},{1,3},{3,1},{5,7},{7,5},{8,10},{10,8},{12,... | collective-permute-start | bytes 393224 | tf_op jit(solution)/shard_map/ppermute | solution.py:47
  195.0 11.7 %collective-permute-start.37 = (bf16[48,1024]{1,0:T(8,128)(2,1)}, bf16[48,1024]{1,0:T(8,128)(2,1)S(1)}, u32[]{:S(2)}, u32[]{:S(2)}) collective-permute-start(bf16[48,1024]{1,0:T(8,128)(2,1)} %shard_map.104), channel_id=1, source_target_pairs={{0,4},{2,6},{4,0},{6,2},{1,5},{3,7},{5,1},{7,3},{8,12},{10,14},{12... | collective-permute-start | bytes 294920 | tf_op jit(solution)/shard_map/ppermute | solution.py:47
  198.9 17.3 %collective-permute-start.25 = (bf16[256,256]{1,0:T(8,128)(2,1)S(1)}, bf16[256,256]{1,0:T(8,128)(2,1)S(1)}, u32[]{:S(2)}, u32[]{:S(2)}) collective-permute-start(bf16[256,256]{1,0:T(8,128)(2,1)S(1)} %copy-done.3), channel_id=1, source_target_pairs={{0,6},{2,4},{4,2},{6,0},{1,7},{3,5},{5,3},{7,1},{8,14},{10,12},{12... | collective-permute-start | bytes 393224 | tf_op jit(solution)/shard_map/ppermute | solution.py:47
  201.0 17.3 %collective-permute-start.24 = (bf16[256,256]{1,0:T(8,128)(2,1)S(1)}, bf16[256,256]{1,0:T(8,128)(2,1)S(1)}, u32[]{:S(2)}, u32[]{:S(2)}) collective-permute-start(bf16[256,256]{1,0:T(8,128)(2,1)S(1)} %copy-done.3), channel_id=1, source_target_pairs={{0,4},{2,6},{4,0},{6,2},{1,5},{3,7},{5,1},{7,3},{8,12},{10,14},{12... | collective-permute-start | bytes 393224 | tf_op jit(solution)/shard_map/ppermute | solution.py:47
  213.1 13.1 %collective-permute-start.41 = (bf16[16,1024]{1,0:T(8,128)(2,1)S(1)}, bf16[16,1024]{1,0:T(8,128)(2,1)S(1)}, u32[]{:S(2)}, u32[]{:S(2)}) collective-permute-start(bf16[16,1024]{1,0:T(8,128)(2,1)S(1)} %get-tuple-element.91), channel_id=1, source_target_pairs={{0,17},{1,16},{16,1},{17,0},{2,19},{3,18},{18,3},{19,2},{4,21},{5,... | collective-permute-start | bytes 98312 | tf_op jit(solution)/shard_map/ppermute | solution.py:47
  215.1 12.5 %collective-permute-start.40 = (bf16[16,1024]{1,0:T(8,128)(2,1)S(1)}, bf16[16,1024]{1,0:T(8,128)(2,1)S(1)}, u32[]{:S(2)}, u32[]{:S(2)}) collective-permute-start(bf16[16,1024]{1,0:T(8,128)(2,1)S(1)} %get-tuple-element.92), channel_id=1, source_target_pairs={{0,16},{1,17},{16,0},{17,1},{2,18},{3,19},{18,2},{19,3},{4,20},{5,... | collective-permute-start | bytes 98312 | tf_op jit(solution)/shard_map/ppermute | solution.py:47
  216.1 11.5 %collective-permute-start.39 = (bf16[16,1024]{1,0:T(8,128)(2,1)S(1)}, bf16[16,1024]{1,0:T(8,128)(2,1)S(1)}, u32[]{:S(2)}, u32[]{:S(2)}) collective-permute-start(bf16[16,1024]{1,0:T(8,128)(2,1)S(1)} %get-tuple-element.93), channel_id=1, source_target_pairs={{0,1},{1,0},{16,17},{17,16},{2,3},{3,2},{18,19},{19,18},{4,5},{5,4... | collective-permute-start | bytes 98312 | tf_op jit(solution)/shard_map/ppermute | solution.py:47
  224.1 11.9 %collective-permute-start.42 = (bf16[256,256]{1,0:T(8,128)(2,1)}, bf16[256,256]{1,0:T(8,128)(2,1)S(1)}, u32[]{:S(2)}, u32[]{:S(2)}) collective-permute-start(bf16[256,256]{1,0:T(8,128)(2,1)} %get-tuple-element.69), channel_id=1, source_target_pairs={{0,1},{1,0},{16,17},{17,16},{2,3},{3,2},{18,19},{19,18},{4,5},{5,4... | collective-permute-start | bytes 393224 | tf_op jit(solution)/shard_map/ppermute | solution.py:47
  237.5 10.9 %all-to-all-start.2 = ((f32[32,1,256]{2,1,0:T(1,128)}), f32[32,1,256]{2,1,0:T(1,128)S(1)}, u32[]{:S(2)}, u32[]{:S(2)}) async-start(f32[32,1,256]{2,1,0:T(1,128)} %reshape.159), calls=%async_computation.2 | async-start | bytes 65536 | tf_op jit(solution)/shard_map/all_to_all | solution.py:455
  250.6 10.9 %collective-permute-start.54 = (f32[16,256]{1,0:T(8,128)S(1)}, f32[16,256]{1,0:T(8,128)S(1)}, u32[]{:S(2)}, u32[]{:S(2)}) collective-permute-start(f32[16,256]{1,0:T(8,128)S(1)} %get-tuple-element.117), channel_id=1, source_target_pairs={{0,1},{1,0},{8,9},{9,8},{16,17},{17,16},{24,25},{25,24},{2,3},{3,2... | collective-permute-start | bytes 49160 | tf_op jit(solution)/shard_map/ppermute | solution.py:47
  253.3 12.9 %all-to-all-start.3 = ((bf16[8,32,448]{2,1,0:T(8,128)(2,1)}), bf16[8,32,448]{2,1,0:T(8,128)(2,1)S(1)}, u32[]{:S(2)}, u32[]{:S(2)}) async-start(bf16[8,32,448]{2,1,0:T(8,128)(2,1)} %copy.48), calls=%async_computation.3 | async-start | bytes 524288 | tf_op jit(solution)/shard_map/all_to_all | solution.py:464
  (79 other events, 609.6 us)

commit v2 on v1

--- a/solution.py
+++ b/solution.py
@@ -97,9 +97,15 @@
         down_part[s] = known[:, plan.features :]
 
 
-def collect(plan, where, *refs):
-    for k in range(plan.quarters):
-        refs[plan.quarters][where[0] ^ k] = refs[k][...]
+def collect(plan, stages, where, *refs):
+    pieces, outs = refs[: plan.quarters], refs[plan.quarters :]
+    for k, piece in enumerate(pieces):
+        source = where[0] ^ k
+        for y, out in zip(stages, outs):
+
+            @pl.when(source // plan.nx == y)
+            def _():
+                out[source % plan.nx] = piece[...]
 
 
 def first_rows(plan, where, *refs):
@@ -216,11 +222,33 @@
         compute(twin)
 
 
+def add_carried(plan, where, *refs):
+    quarter, ic = where[0], where[4]
+    ins, outs, rows = refs[: plan.nz], refs[plan.nz : -1], refs[-1]
+    for j in range(plan.nz):
+        total = 0.0
+        for m in range(plan.nz):
+            total = total + ins[m][:, (j ^ m) * plan.width : ((j ^ m) + 1) * plan.width].astype(F32)
+        rows[:, j * plan.width : (j + 1) * plan.width] = total.astype(BF16)
+    for k, out in enumerate(outs):
+        target = jnp.minimum((quarter ^ k) // plan.nx * plan.nc + ic, plan.sections - 2)
+        out[...] = rows[pl.ds(pl.multiple_of(target * plan.rank, plan.rank), plan.rank), :]
+
+
+def top_rows(plan, where, *refs):
+    grad, act, top_terms, squares = refs
+    for m in range(plan.slots):
+        where_rows = slice(m * plan.positions, (m + 1) * plan.positions)
+        top = nn(act[:, where_rows], grad[where_rows, :])
+        top_terms[m] = top
+        squares[m : m + 1, :] = jnp.full((1, LANES), jnp.sum(top * top), F32)
+
+
 def own_terms(plan, where, *refs):
     quarter, iz, section = where[0], where[1], where[2]
     pieces = refs[: plan.quarters]
-    up_rows, grad, inputs, live, act = refs[plan.quarters : plan.quarters + 5]
-    down_terms, top_terms, squares, carried = refs[plan.quarters + 5 :]
+    up_rows, grad, inputs, live, top_squares = refs[plan.quarters : plan.quarters + 5]
+    down_terms, squares, carried = refs[plan.quarters + 5 :]
     last = section == plan.sections - 1
     for k, piece in enumerate(pieces):
         for m in range(plan.nz):
@@ -241,11 +269,9 @@
     for m in range(plan.slots):
         where_rows = slice(m * plan.positions, (m + 1) * plan.positions)
         down = nn(up_grad[:, where_rows], inputs[where_rows, :])
-        top = nn(act[:, where_rows], grad[where_rows, :])
         down_terms[m] = down
-        top_terms[m] = top
-        total = jnp.sum(down * down) + jnp.where(last, jnp.sum(top * top), 0.0)
-        squares[m : m + 1, :] = jnp.full((1, LANES), total, F32)
+        total = jnp.full((1, LANES), jnp.sum(down * down), F32)
+        squares[m : m + 1, :] = total + jnp.where(last, top_squares[m : m + 1, :], 0.0)
 
 
 def on_device(acts, cotangent, frozen, down_adapter, up_adapter, example_ids, lengths):
@@ -331,19 +357,15 @@
 
     own, twin = {}, {}
 
-    later = cut([outs[0]])
-
     def share(core, pieces, after):
         held = [pieces[0]] + [send_weight(pieces, core, step) for step in range(1, quarters)]
-        (own[core],) = run(collect, held, [shape_of((quarters, block, wide))], after=after)
-        twin[core] = lax.ppermute(own[core], "c", [(core, c) for c in range(nc) if c != core])
-
-    share(nc - 1, pieces, [up_quarter, later[1]])
-
-    def weight_specs(t):
-        y = t // nc
-        spec = pl.BlockSpec((nx, block, wide), lambda i: (y, 0, 0))
-        return [spec, spec]
+        rows = [y for y in range(ny - 1, -1, -1) if y * nc + core > 0]
+        found = run(collect, held, [shape_of((nx, block, wide))] * len(rows), extra=(rows,), after=after)
+        for y, value in zip(rows, found):
+            own[y * nc + core] = value
+            twin[y * nc + core] = lax.ppermute(value, "c", [(core, c) for c in range(nc) if c != core])
+
+    share(nc - 1, pieces, [up_quarter])
 
     finals = {}
 
@@ -351,13 +373,13 @@
         count, height = len(rows), rows[0].shape[0]
         made = run(
             stage_rows,
-            rows + [own[t % nc], twin[t % nc], up_quarter, down_part],
+            rows + [own[t], twin[t], up_quarter, down_part],
             [shape_of((height, width))] * quarters,
             scratch=[
                 pltpu.VMEM((height if count > 1 else 8, wide), BF16),
                 pltpu.VMEM((quarters, height, width), BF16),
             ],
-            specs=[VMEM] * count + weight_specs(t) + [VMEM, VMEM],
+            specs=[VMEM] * count + [VMEM, VMEM] + [VMEM, VMEM],
             extra=(t, count),
             after=after,
         )
@@ -370,6 +392,9 @@
         mine = keep.astype(BF16)
         return [mine] + [xor_permute(mine, "z", nz, m) for m in range(1, nz)]
 
+    top_terms, top_squares = run(
+        top_rows, [cotangent, down_act], [shape_of((slots, rank, features), F32), shape_of((slots, LANES), F32)]
+    )
     marks, sent = {}, {}
     rows = [lead[:, : plan.group].reshape(replicas * plan.group, wide)]
     for t in range(sections - 1, 0, -1):
@@ -379,7 +404,7 @@
             sent[t] = rows[0]
         if t == sections - 1:
             for core in range(nc - 2, -1, -1):
-                share(core, later, [sent[t]])
+                share(core, pieces, [sent[t], top_squares])
     finals[0] = total
     rows = lax.all_to_all(outs[1], ("z", "x"), split_axis=0, concat_axis=0)
     rows = [rows.reshape(-1, wide)]
@@ -392,7 +417,8 @@
 
     seed = jnp.sum(lead[:, plan.group :].astype(F32), axis=0).astype(BF16)
     seed = lax.dynamic_slice_in_dim(seed, replica * block % LANES, block, 1)
-    seed = jnp.where(ic == 1 % nc, seed, lax.ppermute(seed, "c", [(1 % nc, c) for c in range(nc) if c != 1 % nc]))
+    other = lax.ppermute(seed, "c", [(1 % nc, c) for c in range(nc) if c != 1 % nc])
+    seed = jnp.where(ic == 1 % nc, seed, other)
     seeds = [seed] + [xor_permute(seed, ("y", "x"), quarters, k) for k in range(1, quarters)]
     seeds = jnp.stack(seeds)
     home = (1 // nc) * nx
@@ -407,10 +433,10 @@
         height = t * rank
         made = run(
             carry_rows,
-            prefix + [own[t % nc], twin[t % nc], up_quarter, up_part, down_part],
+            prefix + [own[t], twin[t], up_quarter, up_part, down_part],
             [shape_of((height, width))] * nz if split else [shape_of((height, wide))],
             scratch=[pltpu.VMEM((height, width * quarters), BF16)],
-            specs=[VMEM] * count + weight_specs(t) + [VMEM] * 3,
+            specs=[VMEM] * count + [VMEM, VMEM] + [VMEM] * 3,
             extra=(t, count, split),
             after=[sent[sections + 1 - t]],
         )
@@ -421,27 +447,22 @@
             total = total.astype(BF16)
             prefix = [total] + [xor_permute(total, ("y", "x"), quarters, k) for k in range(1, quarters)]
         else:
-            total = made[0].astype(F32).reshape(height, nz, width)
-            for m in range(1, nz):
-                other = xor_permute(made[0], "z", nz, m).astype(F32)
-                total = total + jnp.concatenate(
-                    [other[:, (j ^ m) * width : ((j ^ m) + 1) * width] for j in range(nz)], axis=1
-                ).reshape(height, nz, width)
-            total = total.astype(BF16).reshape(sections - 1, rank, wide)
-            picked = []
-            for k in range(quarters):
-                target = (quarter ^ k) // nx * nc + ic
-                picked.append(
-                    lax.dynamic_index_in_dim(total, jnp.minimum(target, sections - 2), 0, keepdims=False)
-                )
+            others = [xor_permute(made[0], "z", nz, m) for m in range(1, nz)]
+            picked = run(
+                add_carried,
+                [made[0]] + others,
+                [shape_of((rank, wide))] * quarters,
+                scratch=[pltpu.VMEM((height, wide), BF16)],
+                after=[marks[1]],
+            )
             prefix = [picked[0]] + [
                 xor_permute(picked[k], ("y", "x"), quarters, k) for k in range(1, quarters)
             ]
 
-    down_terms, top_terms, own_squares = run(
+    down_terms, own_squares = run(
         own_terms,
-        prefix + [up_rows, cotangent, inputs, live, down_act],
-        [shape_of((slots, rank, features), F32), shape_of((slots, rank, features), F32), shape_of((slots, LANES), F32)],
+        prefix + [up_rows, cotangent, inputs, live, top_squares],
+        [shape_of((slots, rank, features), F32), shape_of((slots, LANES), F32)],
         scratch=[pltpu.VMEM((rank, features), BF16)],
         after=[marks[1]],
     )

time: 268 us -> 267 us (level)
  waiting for transfers between devices: 67.9 us -> 83.1 us
  starting transfers between devices: 105 us -> 91.2 us
    ppermute x52, waiting for transfers between devices: 36.8 us -> 48.9 us  [xor_permute(): return lax.ppermute(value, axes, [(i, i ^ step) for i in range(count)])]
    ppermute x52, starting transfers between devices: 73.1 us -> 63.4 us  [xor_permute(): return lax.ppermute(value, axes, [(i, i ^ step) for i in range(count)])]
    all_to_all x1, waiting for transfers between devices: 6.62 us -> 3.25 us  [on_device(): rows = lax.all_to_all(outs[1], ('z', 'x'), split_axis=0, concat_axis=0)]
    all_to_all x1, waiting for transfers between devices: 0.01 us -> 3.15 us  [on_device(): sums = lax.all_to_all(sums, ('z', 'x'), split_axis=0, concat_axis=0)]
    all_to_all x1, starting transfers between devices: 7.15 us -> 4.4 us  [on_device(): rows = lax.all_to_all(outs[1], ('z', 'x'), split_axis=0, concat_axis=0)]
    unnamed x104 -> x114, local copies, waits for them, and re-layouts: 9.04 us -> 9.98 us
    pallas_call x14 -> x15, Pallas kernels: 62.2 us -> 61.4 us  [local_call(): pl.pallas_call(body, out_shape=shapes, grid=(1,), in_specs=[SMEM] + specs...]
  transfers between devices with their start and end apart: 65 -> 66, of which waited for: 19 -> 21; matrix products, arithmetic and copies ran while one was open for 5% -> 4% of each run, Pallas kernels for 18% -> 18%
where the time goes in v2:
time: 267 us; the launch traced here: 266 us
  starting transfers between devices  91.2 us (34%)
  waiting for transfers between devices  83.1 us (31%)
  Pallas kernels  61.4 us (23%)
  local copies, waits for them, and re-layouts  17.1 us (6%)
  other arithmetic  8.57 us (3%)
  matrix products  3.12 us (1%)
    ppermute x52, starting transfers between devices, xor_permute(): return lax.ppermute(value, axes, [(i, i ^ step) for i in range(count)])  63.4 us
    pallas_call x15, Pallas kernels, local_call(): pl.pallas_call(body, out_shape=shapes, grid=(1,), in_specs=[SMEM] + specs...  61.4 us
    ppermute x52, waiting for transfers between devices, xor_permute(): return lax.ppermute(value, axes, [(i, i ^ step) for i in range(count)])  48.9 us
    all_to_all x1, waiting for transfers between devices, on_device(): lead = lax.all_to_all(outs[0], ('z', 'x'), split_axis=0, concat_axis=0)  17.9 us
    unnamed x114, local copies, waits for them, and re-layouts  9.98 us
    all_to_all x1, waiting for transfers between devices, on_device(): lax.all_to_all(squares, ('y', 'c', 'z', 'x'), split_axis=0, concat_axis=0)  6.92 us
    ppermute x6, starting transfers between devices, send_weight(): return lax.ppermute(pieces[step], ('y', 'c', 'x'), pairs)  6.32 us
  transfers between devices with their start and end apart: 66, of which 21 were waited for; matrix products, arithmetic and copies ran while one was open for 4% of the time, Pallas kernels for 18%

profile of v2, /device:TPU:0, one launch (start us, length us, event | category | flops | bytes accessed | tf_op | source)
XLA Modules:
  0.0 266.2 jit_solution(15070614537498208055)
XLA Ops:
  3.0 3.1 %fusion.2.refs_1_ = bf16[16,512]{1,0:T(8,128)(2,1)S(1)} fusion(bf16[1,16,3584]{2,1,0:T(8,128)(2,1)S(1)} %copy-done, f32[512]{0:T(512)S(1)} %get-tuple-element.116, bf16[1,512,3584]{2,1,0:T(8,128)(2,1)} %param.7), kind=kOutput, calls=%fused_computation.3 | convolution fusion | flops 58753024 | bytes 3803136 | tf_op jit(solution)/shard_map/dot_general | solution.py:18
  13.3 4.9 %shard_map.94 = (bf16[448,1024]{1,0:T(8,128)(2,1)}, bf16[448,1024]{1,0:T(8,128)(2,1)}, bf16[448,1024]{1,0:T(8,128)(2,1)}, bf16[448,1024]{1,0:T(8,128)(2,1)}) custom-call(s32[7]{0:T(128)} %stack.95.at, bf16[16,960]{1,0:T(8,128)(2,1)} %copy-done.23, bf16[16,960]{1,0:T(8,128)(2,1)} %copy-done.24, bf16[16,960]{1,0:T(8,128)(2,1)} %copy-done.25, ...), custom_call_target="tpu_custom_call" | custom-call | tf_op jit(solution)/shard_map/pallas_call | solution.py:31
  20.3 6.4 %collective-permute-start.3 = (bf16[16,4480]{1,0:T(8,128)(2,1)S(1)}, bf16[16,4480]{1,0:T(8,128)(2,1)S(1)}, u32[]{:S(2)}, u32[]{:S(2)}) collective-permute-start(bf16[16,4480]{1,0:T(8,128)(2,1)S(1)} %pad_maximum_fusion.1.refs_1_), channel_id=1, source_target_pairs={{0,8},{8,0},{16,24},{24,16},{1,9},{9,1},{17,25},{25,17},{2,10},{10... | collective-permute-start | bytes 430088 | tf_op jit(solution)/shard_map/ppermute | solution.py:47
  29.2 5.1 %shard_map.95 = (bf16[8,48,1024]{2,1,0:T(8,128)(2,1)}, bf16[8,64,1024]{2,1,0:T(8,128)(2,1)}) custom-call(s32[7]{0:T(128)} %stack.95.at, bf16[448,1024]{1,0:T(8,128)(2,1)} %get-tuple-element.46.refs_0_, bf16[16,960]{1,0:T(8,128)(2,1)} %copy-done.26, bf16[16,960]{1,0:T(8,128)(2,1)} %copy-done.23, bf16[16,960]{1,0:T(8,128)(2,1)} %copy-done.24, ...), custom_call_target="tpu_custom_call" | custom-call | tf_op jit(solution)/shard_map/pallas_call | solution.py:31
  34.3 8.9 %collective-permute-done.4.refs_3_ = bf16[16,4480]{1,0:T(8,128)(2,1)S(1)} collective-permute-done((bf16[16,4480]{1,0:T(8,128)(2,1)S(1)}, bf16[16,4480]{1,0:T(8,128)(2,1)S(1)}, u32[]{:S(2)}, u32[]{:S(2)}) %collective-permute-start.4) | collective-permute-done | bytes 143392 | tf_op jit(solution)/shard_map/ppermute | solution.py:47
  43.2 8.6 %collective-permute-done.5.refs_4_ = bf16[16,4480]{1,0:T(8,128)(2,1)S(1)} collective-permute-done((bf16[16,4480]{1,0:T(8,128)(2,1)S(1)}, bf16[16,4480]{1,0:T(8,128)(2,1)S(1)}, u32[]{:S(2)}, u32[]{:S(2)}) %collective-permute-start.5) | collective-permute-done | bytes 143392 | tf_op jit(solution)/shard_map/ppermute | solution.py:47
  56.0 4.2 %shard_map.97 = (bf16[2,448,1024]{2,1,0:T(8,128)(2,1)}, bf16[2,448,1024]{2,1,0:T(8,128)(2,1)}) custom-call(s32[7]{0:T(128)} %stack.95.at, bf16[4,16,1024]{2,1,0:T(8,128)(2,1)} %get-tuple-element.48.refs_0_.refs_3_.refs_6_.refs_4_.refs_7_, bf16[448,1024]{1,0:T(8,128)(2,1)} %get-tuple-element.49.refs_1_.refs_2_, bf16[448,1024]{1,0:T(8,128)(2,1)} %copy-done.12, ...), custom_call_target="tpu_custom_call" | custom-call | tf_op jit(solution)/shard_map/pallas_call | solution.py:31
  61.5 4.9 %all-to-all-start = ((bf16[8,48,1024]{2,1,0:T(8,128)(2,1)}), bf16[8,48,1024]{2,1,0:T(8,128)(2,1)S(1)}, u32[]{:S(2)}, u32[]{:S(2)}) async-start(bf16[8,48,1024]{2,1,0:T(8,128)(2,1)} %get-tuple-element.47.refs_0_), calls=%async_computation | async-start | bytes 1572864 | tf_op jit(solution)/shard_map/all_to_all | solution.py:335
  70.6 17.9 %all-to-all-done = bf16[8,48,1024]{2,1,0:T(8,128)(2,1)S(1)} async-done(((bf16[8,48,1024]{2,1,0:T(8,128)(2,1)}), bf16[8,48,1024]{2,1,0:T(8,128)(2,1)S(1)}, u32[]{:S(2)}, u32[]{:S(2)}) %all-to-all-start) | async-done | bytes 786464 | tf_op jit(solution)/shard_map/all_to_all | solution.py:335
  90.7 4.3 %shard_map.98 = (bf16[256,256]{1,0:T(8,128)(2,1)}, bf16[256,256]{1,0:T(8,128)(2,1)}, bf16[256,256]{1,0:T(8,128)(2,1)}, bf16[256,256]{1,0:T(8,128)(2,1)}) custom-call(s32[7]{0:T(128)} %stack.95.at, bf16[256,1024]{1,0:T(8,128)(2,1)} %bitcast.108, bf16[2,448,1024]{2,1,0:T(8,128)(2,1)} %get-tuple-element.52.refs_1_.refs_5_.refs_2_, ...), custom_call_target="tpu_custom_call" | custom-call | tf_op jit(solution)/shard_map/pallas_call | solution.py:31
  97.4 4.3 %collective-permute-done.12 = bf16[256,256]{1,0:T(8,128)(2,1)S(1)} collective-permute-done((bf16[256,256]{1,0:T(8,128)(2,1)}, bf16[256,256]{1,0:T(8,128)(2,1)S(1)}, u32[]{:S(2)}, u32[]{:S(2)}) %collective-permute-start.12) | collective-permute-done | bytes 131104 | tf_op jit(solution)/shard_map/ppermute | solution.py:47
  102.8 3.6 %shard_map.99 = (f32[4,16,3584]{2,1,0:T(8,128)}, f32[4,128]{1,0:T(4,128)}) custom-call(s32[7]{0:T(128)} %stack.95.at, bf16[512,3584]{1,0:T(8,128)(2,1)} %refs_6_.1, bf16[16,512]{1,0:T(8,128)(2,1)} %copy-done.19), custom_call_target="tpu_custom_call" | custom-call | tf_op jit(solution)/shard_map/pallas_call | solution.py:31
  107.6 3.5 %shard_map.100.refs_4_.refs_2_.refs_5_ = bf16[2,448,1024]{2,1,0:T(8,128)(2,1)} custom-call(s32[7]{0:T(128)} %stack.95.at, bf16[256,256]{1,0:T(8,128)(2,1)} %add_convert_fusion.1.refs_0_, f32[4,128]{1,0:T(4,128)} %get-tuple-element.58.refs_1_.refs_9_, bf16[448,1024]{1,0:T(8,128)(2,1)} %get-tuple-element.49.refs_1_.refs_2_, ...), custom_call_target="tpu_custom_call" | custom-call | tf_op jit(solution)/shard_map/pallas_call | solution.py:31
  112.6 4.4 %all-to-all-start.1 = ((bf16[8,64,1024]{2,1,0:T(8,128)(2,1)}), bf16[8,64,1024]{2,1,0:T(8,128)(2,1)S(1)}, u32[]{:S(2)}, u32[]{:S(2)}) async-start(bf16[8,64,1024]{2,1,0:T(8,128)(2,1)} %get-tuple-element.78), calls=%async_computation.1 | async-start | bytes 2097152 | tf_op jit(solution)/shard_map/all_to_all | solution.py:409
  120.6 3.1 %collective-permute-done.27 = bf16[16,448]{1,0:T(8,128)(2,1)S(1)} collective-permute-done((bf16[16,448]{1,0:T(8,128)(2,1)S(1)}, bf16[16,448]{1,0:T(8,128)(2,1)S(1)}, u32[]{:S(2)}, u32[]{:S(2)}) %collective-permute-start.27) | collective-permute-done | bytes 14368 | tf_op jit(solution)/shard_map/ppermute | solution.py:420
  132.6 3.1 %collective-permute-start.14 = (bf16[256,256]{1,0:T(8,128)(2,1)S(1)}, bf16[256,256]{1,0:T(8,128)(2,1)S(1)}, u32[]{:S(2)}, u32[]{:S(2)}) collective-permute-start(bf16[256,256]{1,0:T(8,128)(2,1)S(1)} %copy-done.4), channel_id=1, source_target_pairs={{0,4},{2,6},{4,0},{6,2},{1,5},{3,7},{5,1},{7,3},{8,12},{10,14},{12... | collective-permute-start | bytes 393224 | tf_op jit(solution)/shard_map/ppermute | solution.py:47
  137.6 3.3 %shard_map.103 = (bf16[32,256]{1,0:T(8,128)(2,1)}, bf16[32,256]{1,0:T(8,128)(2,1)}, bf16[32,256]{1,0:T(8,128)(2,1)}, bf16[32,256]{1,0:T(8,128)(2,1)}) custom-call(s32[7]{0:T(128)} %stack.95.at, bf16[256,256]{1,0:T(8,128)(2,1)} %add_convert_fusion.1.refs_0_, bf16[16,896]{1,0:T(8,128)(2,1)} %pad_maximum_fusion.4.refs_1_, ...), custom_call_target="tpu_custom_call" | custom-call | tf_op jit(solution)/shard_map/pallas_call | solution.py:31
  142.5 3.3 %all-to-all-done.1 = bf16[8,64,1024]{2,1,0:T(8,128)(2,1)S(1)} async-done(((bf16[8,64,1024]{2,1,0:T(8,128)(2,1)}), bf16[8,64,1024]{2,1,0:T(8,128)(2,1)S(1)}, u32[]{:S(2)}, u32[]{:S(2)}) %all-to-all-start.1) | async-done | bytes 1048608 | tf_op jit(solution)/shard_map/all_to_all | solution.py:409
  146.8 6.1 %shard_map.107 = (bf16[512,256]{1,0:T(8,128)(2,1)}, bf16[512,256]{1,0:T(8,128)(2,1)}, bf16[512,256]{1,0:T(8,128)(2,1)}, bf16[512,256]{1,0:T(8,128)(2,1)}) custom-call(s32[7]{0:T(128)} %stack.95.at, bf16[256,256]{1,0:T(8,128)(2,1)} %add_convert_fusion.1.refs_0_, bf16[512,1024]{1,0:T(8,128)(2,1)} %bitcast.104, ...), custom_call_target="tpu_custom_call" | custom-call | tf_op jit(solution)/shard_map/pallas_call | solution.py:31
  156.5 4.4 %collective-permute-done.31 = bf16[32,256]{1,0:T(8,128)(2,1)S(1)} collective-permute-done((bf16[32,256]{1,0:T(8,128)(2,1)S(1)}, bf16[32,256]{1,0:T(8,128)(2,1)S(1)}, u32[]{:S(2)}, u32[]{:S(2)}) %collective-permute-start.31) | collective-permute-done | bytes 16416 | tf_op jit(solution)/shard_map/ppermute | solution.py:47
  162.2 5.5 %collective-permute-done.15.refs_3_ = bf16[256,256]{1,0:T(8,128)(2,1)S(1)} collective-permute-done((bf16[256,256]{1,0:T(8,128)(2,1)S(1)}, bf16[256,256]{1,0:T(8,128)(2,1)S(1)}, u32[]{:S(2)}, u32[]{:S(2)}) %collective-permute-start.15) | collective-permute-done | bytes 131104 | tf_op jit(solution)/shard_map/ppermute | solution.py:47
  168.6 4.5 %shard_map.101 = (bf16[256,256]{1,0:T(8,128)(2,1)}, bf16[256,256]{1,0:T(8,128)(2,1)}, bf16[256,256]{1,0:T(8,128)(2,1)}, bf16[256,256]{1,0:T(8,128)(2,1)}) custom-call(s32[7]{0:T(128)} %stack.95.at, bf16[256,256]{1,0:T(8,128)(2,1)} %add_convert_fusion.1.refs_0_, bf16[256,256]{1,0:T(8,128)(2,1)} %copy-done.28, bf16[256,256]{1,0:T(8,128)(2,1)} %copy-done.29, ...), custom_call_target="tpu_custom_call" | custom-call | tf_op jit(solution)/shard_map/pallas_call | solution.py:31
  177.9 3.0 %collective-permute-done.35.refs_3_ = bf16[32,256]{1,0:T(8,128)(2,1)S(1)} collective-permute-done((bf16[32,256]{1,0:T(8,128)(2,1)S(1)}, bf16[32,256]{1,0:T(8,128)(2,1)S(1)}, u32[]{:S(2)}, u32[]{:S(2)}) %collective-permute-start.35) | collective-permute-done | bytes 16416 | tf_op jit(solution)/shard_map/ppermute | solution.py:47
  190.6 3.4 %shard_map.104.refs_1_ = bf16[48,1024]{1,0:T(8,128)(2,1)} custom-call(s32[7]{0:T(128)} %stack.95.at, bf16[256,256]{1,0:T(8,128)(2,1)} %copy-done.7, bf16[32,256]{1,0:T(8,128)(2,1)} %copy-done.41, bf16[32,256]{1,0:T(8,128)(2,1)} %copy-done.45, bf16[32,256]{1,0:T(8,128)(2,1)} %copy-done.46, bf16[32,256]{1,0:T(8,128)(2,1)} %copy-done.47, ...), custom_call_target="tpu_custom_call" | custom-call | tf_op jit(solution)/shard_map/pallas_call | solution.py:31
  198.5 4.4 %shard_map.108 = (bf16[256,256]{1,0:T(8,128)(2,1)}, bf16[256,256]{1,0:T(8,128)(2,1)}, bf16[256,256]{1,0:T(8,128)(2,1)}, bf16[256,256]{1,0:T(8,128)(2,1)}) custom-call(s32[7]{0:T(128)} %stack.95.at, bf16[256,256]{1,0:T(8,128)(2,1)} %copy-done.7, bf16[256,256]{1,0:T(8,128)(2,1)} %bitcast.118, bf16[256,256]{1,0:T(8,128)(2,1)} %copy-done.32, ...), custom_call_target="tpu_custom_call" | custom-call | tf_op jit(solution)/shard_map/pallas_call | solution.py:31
  211.1 4.4 %shard_map.102 = (bf16[256,256]{1,0:T(8,128)(2,1)}, bf16[256,256]{1,0:T(8,128)(2,1)}, bf16[256,256]{1,0:T(8,128)(2,1)}, bf16[256,256]{1,0:T(8,128)(2,1)}) custom-call(s32[7]{0:T(128)} %stack.95.at, bf16[256,256]{1,0:T(8,128)(2,1)} %copy-done.7, bf16[256,256]{1,0:T(8,128)(2,1)} %copy-done.27, bf16[256,256]{1,0:T(8,128)(2,1)} %copy-done.30, ...), custom_call_target="tpu_custom_call" | custom-call | tf_op jit(solution)/shard_map/pallas_call | solution.py:31
  226.0 6.0 %shard_map.106 = (f32[4,16,3584]{2,1,0:T(8,128)}, f32[4,128]{1,0:T(4,128)}) custom-call(s32[7]{0:T(128)} %stack.95.at, bf16[256,256]{1,0:T(8,128)(2,1)} %get-tuple-element.64.refs_0_, bf16[16,1024]{1,0:T(8,128)(2,1)} %get-tuple-element.70.refs_1_, bf16[16,1024]{1,0:T(8,128)(2,1)} %copy-done.42, bf16[16,1024]{1,0:T(8,128)(2,1)} %copy-done.43, ...), custom_call_target="tpu_custom_call" | custom-call | tf_op jit(solution)/shard_map/pallas_call | solution.py:31
  234.5 3.5 %all-to-all-start.2 = ((f32[32,1,256]{2,1,0:T(1,128)}), f32[32,1,256]{2,1,0:T(1,128)S(1)}, u32[]{:S(2)}, u32[]{:S(2)}) async-start(f32[32,1,256]{2,1,0:T(1,128)} %reshape.146), calls=%async_computation.2 | async-start | bytes 65536 | tf_op jit(solution)/shard_map/all_to_all | solution.py:476
  238.4 6.9 %all-to-all-done.2 = f32[32,1,256]{2,1,0:T(1,128)S(1)} async-done(((f32[32,1,256]{2,1,0:T(1,128)}), f32[32,1,256]{2,1,0:T(1,128)S(1)}, u32[]{:S(2)}, u32[]{:S(2)}) %all-to-all-start.2) | async-done | bytes 32800 | tf_op jit(solution)/shard_map/all_to_all | solution.py:476
  253.2 3.4 %all-to-all-start.3 = ((bf16[8,32,448]{2,1,0:T(8,128)(2,1)}), bf16[8,32,448]{2,1,0:T(8,128)(2,1)S(1)}, u32[]{:S(2)}, u32[]{:S(2)}) async-start(bf16[8,32,448]{2,1,0:T(8,128)(2,1)} %copy.48), calls=%async_computation.3 | async-start | bytes 524288 | tf_op jit(solution)/shard_map/all_to_all | solution.py:485
  257.3 3.1 %collective-permute-start.61 = (f32[16,256]{1,0:T(8,128)S(1)}, f32[16,256]{1,0:T(8,128)S(1)}, u32[]{:S(2)}, u32[]{:S(2)}) collective-permute-start(f32[16,256]{1,0:T(8,128)S(1)} %get-tuple-element.103), channel_id=1, source_target_pairs={{0,25},{1,24},{8,17},{9,16},{16,9},{17,8},{24,1},{25,0},{2,27},{3,... | collective-permute-start | bytes 49160 | tf_op jit(solution)/shard_map/ppermute | solution.py:47
  262.3 3.1 %all-to-all-done.3 = bf16[8,32,448]{2,1,0:T(8,128)(2,1)S(1)} async-done(((bf16[8,32,448]{2,1,0:T(8,128)(2,1)}), bf16[8,32,448]{2,1,0:T(8,128)(2,1)S(1)}, u32[]{:S(2)}, u32[]{:S(2)}) %all-to-all-start.3) | async-done | bytes 229408 | tf_op jit(solution)/shard_map/all_to_all | solution.py:485
  (304 shorter events, 105.8 us)
Async XLA Ops:
  18.1 36.4 %collective-permute-start.6 = (bf16[448,1024]{1,0:T(8,128)(2,1)}, bf16[448,1024]{1,0:T(8,128)(2,1)S(1)}, u32[]{:S(2)}, u32[]{:S(2)}) collective-permute-start(bf16[448,1024]{1,0:T(8,128)(2,1)} %get-tuple-element.46.refs_0_), channel_id=1, source_target_pairs={{8,9},{9,8},{24,25},{25,24},{10,11},{11,10},{26,27},{27,26},{12,13... | collective-permute-start | bytes 2752520 | tf_op jit(solution)/shard_map/ppermute | solution.py:346
  18.8 35.7 %collective-permute-start.7 = (bf16[448,1024]{1,0:T(8,128)(2,1)}, bf16[448,1024]{1,0:T(8,128)(2,1)S(1)}, u32[]{:S(2)}, u32[]{:S(2)}) collective-permute-start(bf16[448,1024]{1,0:T(8,128)(2,1)} %get-tuple-element.50), channel_id=1, source_target_pairs={{8,24},{9,25},{24,8},{25,9},{10,26},{11,27},{26,10},{27,11},{12,28... | collective-permute-start | bytes 2752520 | tf_op jit(solution)/shard_map/ppermute | solution.py:346
  19.6 34.9 %collective-permute-start.8 = (bf16[448,1024]{1,0:T(8,128)(2,1)}, bf16[448,1024]{1,0:T(8,128)(2,1)S(1)}, u32[]{:S(2)}, u32[]{:S(2)}) collective-permute-start(bf16[448,1024]{1,0:T(8,128)(2,1)} %get-tuple-element.51), channel_id=1, source_target_pairs={{8,25},{9,24},{24,9},{25,8},{10,27},{11,26},{26,11},{27,10},{12,29... | collective-permute-start | bytes 2752520 | tf_op jit(solution)/shard_map/ppermute | solution.py:346
  26.8 16.5 %collective-permute-start.4 = (bf16[16,4480]{1,0:T(8,128)(2,1)S(1)}, bf16[16,4480]{1,0:T(8,128)(2,1)S(1)}, u32[]{:S(2)}, u32[]{:S(2)}) collective-permute-start(bf16[16,4480]{1,0:T(8,128)(2,1)S(1)} %pad_maximum_fusion.1.refs_1_), channel_id=1, source_target_pairs={{0,16},{8,24},{16,0},{24,8},{1,17},{9,25},{17,1},{25,9},{2,18},{10... | collective-permute-start | bytes 430088 | tf_op jit(solution)/shard_map/ppermute | solution.py:47
  27.8 24.1 %collective-permute-start.5 = (bf16[16,4480]{1,0:T(8,128)(2,1)S(1)}, bf16[16,4480]{1,0:T(8,128)(2,1)S(1)}, u32[]{:S(2)}, u32[]{:S(2)}) collective-permute-start(bf16[16,4480]{1,0:T(8,128)(2,1)S(1)} %pad_maximum_fusion.1.refs_1_), channel_id=1, source_target_pairs={{0,24},{8,16},{16,8},{24,0},{1,25},{9,17},{17,9},{25,1},{2,26},{10... | collective-permute-start | bytes 430088 | tf_op jit(solution)/shard_map/ppermute | solution.py:47
  60.2 29.2 %collective-permute-start.9 = (bf16[2,448,1024]{2,1,0:T(8,128)(2,1)}, bf16[2,448,1024]{2,1,0:T(8,128)(2,1)S(1)}, u32[]{:S(2)}, u32[]{:S(2)}) collective-permute-start(bf16[2,448,1024]{2,1,0:T(8,128)(2,1)} %get-tuple-element.52.refs_1_.refs_5_.refs_2_), channel_id=1, source_target_pairs={{8,0},{9,1},{10,2},{11,3},{12,4},{13,5},{14,6},{15,7},{24,16},{25,... | collective-permute-start | bytes 5505032 | tf_op jit(solution)/shard_map/ppermute | solution.py:366
  61.5 27.0 %all-to-all-start = ((bf16[8,48,1024]{2,1,0:T(8,128)(2,1)}), bf16[8,48,1024]{2,1,0:T(8,128)(2,1)S(1)}, u32[]{:S(2)}, u32[]{:S(2)}) async-start(bf16[8,48,1024]{2,1,0:T(8,128)(2,1)} %get-tuple-element.47.refs_0_), calls=%async_computation | async-start | bytes 1572864 | tf_op jit(solution)/shard_map/all_to_all | solution.py:335
  66.4 41.2 %collective-permute-start.16 = (bf16[448,1024]{1,0:T(8,128)(2,1)}, bf16[448,1024]{1,0:T(8,128)(2,1)}, u32[]{:S(2)}, u32[]{:S(2)}) collective-permute-start(bf16[448,1024]{1,0:T(8,128)(2,1)} %get-tuple-element.46.refs_0_), channel_id=1, source_target_pairs={{16,17},{17,16},{18,19},{19,18},{20,21},{21,20},{22,23},{23,22}} | collective-permute-start | bytes 2752520 | tf_op jit(solution)/shard_map/ppermute | solution.py:346
  68.0 39.6 %collective-permute-start.17 = (bf16[448,1024]{1,0:T(8,128)(2,1)}, bf16[448,1024]{1,0:T(8,128)(2,1)}, u32[]{:S(2)}, u32[]{:S(2)}) collective-permute-start(bf16[448,1024]{1,0:T(8,128)(2,1)} %get-tuple-element.50), channel_id=1, source_target_pairs={{16,0},{17,1},{18,2},{19,3},{20,4},{21,5},{22,6},{23,7}} | collective-permute-start | bytes 2752520 | tf_op jit(solution)/shard_map/ppermute | solution.py:346
  69.3 38.4 %collective-permute-start.18 = (bf16[448,1024]{1,0:T(8,128)(2,1)}, bf16[448,1024]{1,0:T(8,128)(2,1)}, u32[]{:S(2)}, u32[]{:S(2)}) collective-permute-start(bf16[448,1024]{1,0:T(8,128)(2,1)} %get-tuple-element.51), channel_id=1, source_target_pairs={{16,1},{17,0},{18,3},{19,2},{20,5},{21,4},{22,7},{23,6}} | collective-permute-start | bytes 2752520 | tf_op jit(solution)/shard_map/ppermute | solution.py:346
  111.2 25.2 %collective-permute-start.19 = (bf16[2,448,1024]{2,1,0:T(8,128)(2,1)}, bf16[2,448,1024]{2,1,0:T(8,128)(2,1)S(1)}, u32[]{:S(2)}, u32[]{:S(2)}) collective-permute-start(bf16[2,448,1024]{2,1,0:T(8,128)(2,1)} %shard_map.100.refs_4_.refs_2_.refs_5_), channel_id=1, source_target_pairs={{0,8},{1,9},{2,10},{3,11},{4,12},{5,13},{6,14},{7,15},{16,24},{17,... | collective-permute-start | bytes 5505032 | tf_op jit(solution)/shard_map/ppermute | solution.py:366
  112.6 33.2 %all-to-all-start.1 = ((bf16[8,64,1024]{2,1,0:T(8,128)(2,1)}), bf16[8,64,1024]{2,1,0:T(8,128)(2,1)S(1)}, u32[]{:S(2)}, u32[]{:S(2)}) async-start(bf16[8,64,1024]{2,1,0:T(8,128)(2,1)} %get-tuple-element.78), calls=%async_computation.1 | async-start | bytes 2097152 | tf_op jit(solution)/shard_map/all_to_all | solution.py:409
  117.0 86.0 %collective-permute-start.26 = (bf16[2,448,1024]{2,1,0:T(8,128)(2,1)}, bf16[2,448,1024]{2,1,0:T(8,128)(2,1)}, u32[]{:S(2)}, u32[]{:S(2)}) collective-permute-start(bf16[2,448,1024]{2,1,0:T(8,128)(2,1)} %get-tuple-element.63.refs_4_), channel_id=1, source_target_pairs={{8,0},{9,1},{10,2},{11,3},{12,4},{13,5},{14,6},{15,7},{24,16},{25,... | collective-permute-start | bytes 5505032 | tf_op jit(solution)/shard_map/ppermute | solution.py:366
  131.0 21.9 %collective-permute-start.13 = (bf16[256,256]{1,0:T(8,128)(2,1)S(1)}, bf16[256,256]{1,0:T(8,128)(2,1)S(1)}, u32[]{:S(2)}, u32[]{:S(2)}) collective-permute-start(bf16[256,256]{1,0:T(8,128)(2,1)S(1)} %copy-done.4), channel_id=1, source_target_pairs={{0,2},{2,0},{4,6},{6,4},{1,3},{3,1},{5,7},{7,5},{8,10},{10,8},{12,... | collective-permute-start | bytes 393224 | tf_op jit(solution)/shard_map/ppermute | solution.py:47
  132.6 21.7 %collective-permute-start.14 = (bf16[256,256]{1,0:T(8,128)(2,1)S(1)}, bf16[256,256]{1,0:T(8,128)(2,1)S(1)}, u32[]{:S(2)}, u32[]{:S(2)}) collective-permute-start(bf16[256,256]{1,0:T(8,128)(2,1)S(1)} %copy-done.4), channel_id=1, source_target_pairs={{0,4},{2,6},{4,0},{6,2},{1,5},{3,7},{5,1},{7,3},{8,12},{10,14},{12... | collective-permute-start | bytes 393224 | tf_op jit(solution)/shard_map/ppermute | solution.py:47
  140.9 15.2 %collective-permute-start.33 = (bf16[32,256]{1,0:T(8,128)(2,1)}, bf16[32,256]{1,0:T(8,128)(2,1)S(1)}, u32[]{:S(2)}, u32[]{:S(2)}) collective-permute-start(bf16[32,256]{1,0:T(8,128)(2,1)} %get-tuple-element.69), channel_id=1, source_target_pairs={{0,6},{2,4},{4,2},{6,0},{1,7},{3,5},{5,3},{7,1},{8,14},{10,12},{12... | collective-permute-start | bytes 49160 | tf_op jit(solution)/shard_map/ppermute | solution.py:47
  141.0 15.5 %collective-permute-start.32 = (bf16[32,256]{1,0:T(8,128)(2,1)}, bf16[32,256]{1,0:T(8,128)(2,1)S(1)}, u32[]{:S(2)}, u32[]{:S(2)}) collective-permute-start(bf16[32,256]{1,0:T(8,128)(2,1)} %get-tuple-element.68), channel_id=1, source_target_pairs={{0,4},{2,6},{4,0},{6,2},{1,5},{3,7},{5,1},{7,3},{8,12},{10,14},{12... | collective-permute-start | bytes 49160 | tf_op jit(solution)/shard_map/ppermute | solution.py:47
  152.9 20.1 %collective-permute-start.48 = (bf16[512,256]{1,0:T(8,128)(2,1)}, bf16[512,256]{1,0:T(8,128)(2,1)S(1)}, u32[]{:S(2)}, u32[]{:S(2)}) collective-permute-start(bf16[512,256]{1,0:T(8,128)(2,1)} %get-tuple-element.82), channel_id=1, source_target_pairs={{0,17},{1,16},{16,1},{17,0},{2,19},{3,18},{18,3},{19,2},{4,21},{5,... | collective-permute-start | bytes 786440 | tf_op jit(solution)/shard_map/ppermute | solution.py:47
  154.3 20.0 %collective-permute-start.47 = (bf16[512,256]{1,0:T(8,128)(2,1)}, bf16[512,256]{1,0:T(8,128)(2,1)S(1)}, u32[]{:S(2)}, u32[]{:S(2)}) collective-permute-start(bf16[512,256]{1,0:T(8,128)(2,1)} %get-tuple-element.81), channel_id=1, source_target_pairs={{0,16},{1,17},{16,0},{17,1},{2,18},{3,19},{18,2},{19,3},{4,20},{5,... | collective-permute-start | bytes 786440 | tf_op jit(solution)/shard_map/ppermute | solution.py:47
  156.0 19.7 %collective-permute-start.46 = (bf16[512,256]{1,0:T(8,128)(2,1)}, bf16[512,256]{1,0:T(8,128)(2,1)S(1)}, u32[]{:S(2)}, u32[]{:S(2)}) collective-permute-start(bf16[512,256]{1,0:T(8,128)(2,1)} %get-tuple-element.80), channel_id=1, source_target_pairs={{0,1},{1,0},{16,17},{17,16},{2,3},{3,2},{18,19},{19,18},{4,5},{5,4... | collective-permute-start | bytes 786440 | tf_op jit(solution)/shard_map/ppermute | solution.py:47
  180.9 13.0 %collective-permute-start.49 = (bf16[256,256]{1,0:T(8,128)(2,1)S(1)}, bf16[256,256]{1,0:T(8,128)(2,1)S(1)}, u32[]{:S(2)}, u32[]{:S(2)}) collective-permute-start(bf16[256,256]{1,0:T(8,128)(2,1)S(1)} %bitcast.115), channel_id=1, source_target_pairs={{0,2},{2,0},{4,6},{6,4},{1,3},{3,1},{5,7},{7,5},{8,10},{10,8},{12,... | collective-permute-start | bytes 393224 | tf_op jit(solution)/shard_map/ppermute | solution.py:47
  181.0 13.9 %collective-permute-start.50 = (bf16[256,256]{1,0:T(8,128)(2,1)S(1)}, bf16[256,256]{1,0:T(8,128)(2,1)S(1)}, u32[]{:S(2)}, u32[]{:S(2)}) collective-permute-start(bf16[256,256]{1,0:T(8,128)(2,1)S(1)} %bitcast.116), channel_id=1, source_target_pairs={{0,4},{2,6},{4,0},{6,2},{1,5},{3,7},{5,1},{7,3},{8,12},{10,14},{12... | collective-permute-start | bytes 393224 | tf_op jit(solution)/shard_map/ppermute | solution.py:47
  182.3 15.6 %collective-permute-start.51 = (bf16[256,256]{1,0:T(8,128)(2,1)S(1)}, bf16[256,256]{1,0:T(8,128)(2,1)S(1)}, u32[]{:S(2)}, u32[]{:S(2)}) collective-permute-start(bf16[256,256]{1,0:T(8,128)(2,1)S(1)} %bitcast.117), channel_id=1, source_target_pairs={{0,6},{2,4},{4,2},{6,0},{1,7},{3,5},{5,3},{7,1},{8,14},{10,12},{12... | collective-permute-start | bytes 393224 | tf_op jit(solution)/shard_map/ppermute | solution.py:47
  190.0 18.1 %collective-permute-start.23 = (bf16[256,256]{1,0:T(8,128)(2,1)S(1)}, bf16[256,256]{1,0:T(8,128)(2,1)S(1)}, u32[]{:S(2)}, u32[]{:S(2)}) collective-permute-start(bf16[256,256]{1,0:T(8,128)(2,1)S(1)} %add_convert_fusion.refs_0_), channel_id=1, source_target_pairs={{0,2},{2,0},{4,6},{6,4},{1,3},{3,1},{5,7},{7,5},{8,10},{10,8},{12,... | collective-permute-start | bytes 393224 | tf_op jit(solution)/shard_map/ppermute | solution.py:47
  194.0 14.7 %collective-permute-start.24 = (bf16[256,256]{1,0:T(8,128)(2,1)}, bf16[256,256]{1,0:T(8,128)(2,1)S(1)}, u32[]{:S(2)}, u32[]{:S(2)}) collective-permute-start(bf16[256,256]{1,0:T(8,128)(2,1)} %copy-done.7), channel_id=1, source_target_pairs={{0,4},{2,6},{4,0},{6,2},{1,5},{3,7},{5,1},{7,3},{8,12},{10,14},{12... | collective-permute-start | bytes 393224 | tf_op jit(solution)/shard_map/ppermute | solution.py:47
  194.8 13.9 %collective-permute-start.25 = (bf16[256,256]{1,0:T(8,128)(2,1)}, bf16[256,256]{1,0:T(8,128)(2,1)S(1)}, u32[]{:S(2)}, u32[]{:S(2)}) collective-permute-start(bf16[256,256]{1,0:T(8,128)(2,1)} %copy-done.7), channel_id=1, source_target_pairs={{0,6},{2,4},{4,2},{6,0},{1,7},{3,5},{5,3},{7,1},{8,14},{10,12},{12... | collective-permute-start | bytes 393224 | tf_op jit(solution)/shard_map/ppermute | solution.py:47
  203.0 17.4 %collective-permute-start.54 = (bf16[256,256]{1,0:T(8,128)(2,1)}, bf16[256,256]{1,0:T(8,128)(2,1)S(1)}, u32[]{:S(2)}, u32[]{:S(2)}) collective-permute-start(bf16[256,256]{1,0:T(8,128)(2,1)} %get-tuple-element.86), channel_id=1, source_target_pairs={{0,17},{1,16},{16,1},{17,0},{2,19},{3,18},{18,3},{19,2},{4,21},{5,... | collective-permute-start | bytes 393224 | tf_op jit(solution)/shard_map/ppermute | solution.py:47
  206.7 14.8 %collective-permute-start.53 = (bf16[256,256]{1,0:T(8,128)(2,1)}, bf16[256,256]{1,0:T(8,128)(2,1)S(1)}, u32[]{:S(2)}, u32[]{:S(2)}) collective-permute-start(bf16[256,256]{1,0:T(8,128)(2,1)} %get-tuple-element.85), channel_id=1, source_target_pairs={{0,16},{1,17},{16,0},{17,1},{2,18},{3,19},{18,2},{19,3},{4,20},{5,... | collective-permute-start | bytes 393224 | tf_op jit(solution)/shard_map/ppermute | solution.py:47
  208.1 13.4 %collective-permute-start.52 = (bf16[256,256]{1,0:T(8,128)(2,1)}, bf16[256,256]{1,0:T(8,128)(2,1)S(1)}, u32[]{:S(2)}, u32[]{:S(2)}) collective-permute-start(bf16[256,256]{1,0:T(8,128)(2,1)} %get-tuple-element.84), channel_id=1, source_target_pairs={{0,1},{1,0},{16,17},{17,16},{2,3},{3,2},{18,19},{19,18},{4,5},{5,4... | collective-permute-start | bytes 393224 | tf_op jit(solution)/shard_map/ppermute | solution.py:47
  221.9 11.2 %collective-permute-start.45 = (bf16[256,256]{1,0:T(8,128)(2,1)}, bf16[256,256]{1,0:T(8,128)(2,1)S(1)}, u32[]{:S(2)}, u32[]{:S(2)}) collective-permute-start(bf16[256,256]{1,0:T(8,128)(2,1)} %get-tuple-element.77), channel_id=1, source_target_pairs={{0,17},{1,16},{16,1},{17,0},{2,19},{3,18},{18,3},{19,2},{4,21},{5,... | collective-permute-start | bytes 393224 | tf_op jit(solution)/shard_map/ppermute | solution.py:47
  248.2 12.2 %collective-permute-start.57 = (f32[16,256]{1,0:T(8,128)S(1)}, f32[16,256]{1,0:T(8,128)S(1)}, u32[]{:S(2)}, u32[]{:S(2)}) collective-permute-start(f32[16,256]{1,0:T(8,128)S(1)} %get-tuple-element.107), channel_id=1, source_target_pairs={{0,9},{1,8},{8,1},{9,0},{16,25},{17,24},{24,17},{25,16},{2,11},{3,... | collective-permute-start | bytes 49160 | tf_op jit(solution)/shard_map/ppermute | solution.py:47
  253.2 12.2 %all-to-all-start.3 = ((bf16[8,32,448]{2,1,0:T(8,128)(2,1)}), bf16[8,32,448]{2,1,0:T(8,128)(2,1)S(1)}, u32[]{:S(2)}, u32[]{:S(2)}) async-start(bf16[8,32,448]{2,1,0:T(8,128)(2,1)} %copy.48), calls=%async_computation.3 | async-start | bytes 524288 | tf_op jit(solution)/shard_map/all_to_all | solution.py:485
  (85 other events, 710.8 us)

commit v3 on v2

--- a/solution.py
+++ b/solution.py
@@ -112,12 +112,13 @@
     iz, section, iy, ic, ix, replica = where[1], where[2], where[3], where[4], where[5], where[6]
     tokens = plan.slots * plan.positions
     known_acts = refs[: plan.sections]
-    grad, weight, up_rows, own_down, low_out, high_out, act, rows, seeds = refs[plan.sections :]
+    grad, weight, up_rows, own_down, live, low_out, high_out, act, rows, seeds = refs[plan.sections :]
     for j, known in enumerate(known_acts):
         act[section ^ j] = known[...]
     for i in range(plan.half):
         start = pl.multiple_of((ic * plan.half + i) * plan.positions, plan.positions)
         left = jnp.concatenate([act[s, :, pl.ds(start, plan.positions)] for s in range(plan.sections - 1)], axis=0)
+        left = (left.astype(F32) * live[:, pl.ds(start, plan.positions)]).astype(BF16)
         for m in range(plan.nz):
             lanes = pl.multiple_of((iz ^ m) * plan.part, LANES)
             right = grad[pl.ds(start, plan.positions), pl.ds(lanes, plan.part)]
@@ -307,10 +308,11 @@
     live = live.astype(F32).reshape(1, tokens)
     clip_scale = math.sqrt(2.0 * rank * features) / math.sqrt(replicas * slots)
 
-    down_act = (nt(down_rows, inputs).astype(BF16).astype(F32) * live).astype(BF16)
+    all_act = nt(down_rows, inputs).astype(BF16)
+    down_act = (all_act.astype(F32) * live).astype(BF16)
     own_up = lax.dynamic_slice_in_dim(up_rows, replica * block, block, 1)
     own_down = lax.dynamic_slice_in_dim(down_rows, replica * block, block, 1)
-    act_known = jnp.concatenate([down_act, own_up], axis=1)
+    act_known = jnp.concatenate([all_act, own_up], axis=1)
     act_all = [act_known] + [xor_permute(act_known, ("y", "c"), sections, j) for j in range(1, sections)]
 
     def cut(after):
@@ -320,7 +322,7 @@
 
     outs = run(
         first_rows,
-        act_all + [cotangent, weight, up_rows, own_down],
+        act_all + [cotangent, weight, up_rows, own_down, live],
         [
             shape_of((replicas, plan.group + rank, wide)),
             shape_of((replicas, (sections - 2) * plan.group, wide)),

time: 267 us -> 268 us (level)
    unnamed x114 -> x112, local copies, waits for them, and re-layouts: 9.98 us -> 9.97 us
where the time goes in v3:
time: 268 us; the launch traced here: 267 us
  starting transfers between devices  91.2 us (34%)
  waiting for transfers between devices  83.2 us (31%)
  Pallas kernels  61.4 us (23%)
  local copies, waits for them, and re-layouts  17.1 us (6%)
  other arithmetic  8.56 us (3%)
  matrix products  3.73 us (1%)
    ppermute x52, starting transfers between devices, xor_permute(): return lax.ppermute(value, axes, [(i, i ^ step) for i in range(count)])  63.4 us
    pallas_call x15, Pallas kernels, local_call(): pl.pallas_call(body, out_shape=shapes, grid=(1,), in_specs=[SMEM] + specs...  61.4 us
    ppermute x52, waiting for transfers between devices, xor_permute(): return lax.ppermute(value, axes, [(i, i ^ step) for i in range(count)])  48.9 us
    all_to_all x1, waiting for transfers between devices, on_device(): lead = lax.all_to_all(outs[0], ('z', 'x'), split_axis=0, concat_axis=0)  17.9 us
    unnamed x112, local copies, waits for them, and re-layouts  9.97 us
    all_to_all x1, waiting for transfers between devices, on_device(): lax.all_to_all(squares, ('y', 'c', 'z', 'x'), split_axis=0, concat_axis=0)  6.92 us
    ppermute x6, starting transfers between devices, send_weight(): return lax.ppermute(pieces[step], ('y', 'c', 'x'), pairs)  6.32 us
  transfers between devices with their start and end apart: 66, of which 21 were waited for; matrix products, arithmetic and copies ran while one was open for 4% of the time, Pallas kernels for 18%

profile of v3, /device:TPU:0, one launch (start us, length us, event | category | flops | bytes accessed | tf_op | source)
XLA Modules:
  0.0 266.8 jit_solution(1996766608970849218)
XLA Ops:
  3.0 3.7 %multiply_convert_fusion = (bf16[16,512]{1,0:T(8,128)(2,1)}, bf16[16,512]{1,0:T(8,128)(2,1)S(1)}) fusion(f32[512]{0:T(512)S(1)} %get-tuple-element.115, bf16[1,512,3584]{2,1,0:T(8,128)(2,1)} %param.7, bf16[1,16,3584]{2,1,0:T(8,128)(2,1)S(1)} %copy-done), kind=kOutput, calls=%fused_computation.36 | convolution fusion | flops 58753024 | bytes 3819520 | tf_op jit(solution)/shard_map/dot_general | solution.py:18
  13.8 4.9 %shard_map.94 = (bf16[448,1024]{1,0:T(8,128)(2,1)}, bf16[448,1024]{1,0:T(8,128)(2,1)}, bf16[448,1024]{1,0:T(8,128)(2,1)}, bf16[448,1024]{1,0:T(8,128)(2,1)}) custom-call(s32[7]{0:T(128)} %stack.95.at, bf16[16,960]{1,0:T(8,128)(2,1)} %copy-done.22, bf16[16,960]{1,0:T(8,128)(2,1)} %copy-done.23, bf16[16,960]{1,0:T(8,128)(2,1)} %copy-done.24, ...), custom_call_target="tpu_custom_call" | custom-call | tf_op jit(solution)/shard_map/pallas_call | solution.py:31
  20.9 6.4 %collective-permute-start.3 = (bf16[16,4480]{1,0:T(8,128)(2,1)S(1)}, bf16[16,4480]{1,0:T(8,128)(2,1)S(1)}, u32[]{:S(2)}, u32[]{:S(2)}) collective-permute-start(bf16[16,4480]{1,0:T(8,128)(2,1)S(1)} %pad_maximum_fusion.1.refs_1_), channel_id=1, source_target_pairs={{0,8},{8,0},{16,24},{24,16},{1,9},{9,1},{17,25},{25,17},{2,10},{10... | collective-permute-start | bytes 430088 | tf_op jit(solution)/shard_map/ppermute | solution.py:47
  29.8 5.1 %shard_map.95 = (bf16[8,48,1024]{2,1,0:T(8,128)(2,1)}, bf16[8,64,1024]{2,1,0:T(8,128)(2,1)}) custom-call(s32[7]{0:T(128)} %stack.95.at, bf16[448,1024]{1,0:T(8,128)(2,1)} %get-tuple-element.46.refs_0_, bf16[16,960]{1,0:T(8,128)(2,1)} %copy-done.25, bf16[16,960]{1,0:T(8,128)(2,1)} %copy-done.22, bf16[16,960]{1,0:T(8,128)(2,1)} %copy-done.23, ...), custom_call_target="tpu_custom_call" | custom-call | tf_op jit(solution)/shard_map/pallas_call | solution.py:31
  34.9 8.9 %collective-permute-done.4.refs_3_ = bf16[16,4480]{1,0:T(8,128)(2,1)S(1)} collective-permute-done((bf16[16,4480]{1,0:T(8,128)(2,1)S(1)}, bf16[16,4480]{1,0:T(8,128)(2,1)S(1)}, u32[]{:S(2)}, u32[]{:S(2)}) %collective-permute-start.4) | collective-permute-done | bytes 143392 | tf_op jit(solution)/shard_map/ppermute | solution.py:47
  43.8 8.6 %collective-permute-done.5.refs_4_ = bf16[16,4480]{1,0:T(8,128)(2,1)S(1)} collective-permute-done((bf16[16,4480]{1,0:T(8,128)(2,1)S(1)}, bf16[16,4480]{1,0:T(8,128)(2,1)S(1)}, u32[]{:S(2)}, u32[]{:S(2)}) %collective-permute-start.5) | collective-permute-done | bytes 143392 | tf_op jit(solution)/shard_map/ppermute | solution.py:47
  56.6 4.2 %shard_map.97 = (bf16[2,448,1024]{2,1,0:T(8,128)(2,1)}, bf16[2,448,1024]{2,1,0:T(8,128)(2,1)}) custom-call(s32[7]{0:T(128)} %stack.95.at, bf16[4,16,1024]{2,1,0:T(8,128)(2,1)} %get-tuple-element.48.refs_0_.refs_3_.refs_6_.refs_4_.refs_7_, bf16[448,1024]{1,0:T(8,128)(2,1)} %get-tuple-element.49.refs_1_.refs_2_, bf16[448,1024]{1,0:T(8,128)(2,1)} %copy-done.12, ...), custom_call_target="tpu_custom_call" | custom-call | tf_op jit(solution)/shard_map/pallas_call | solution.py:31
  62.1 4.9 %all-to-all-start = ((bf16[8,48,1024]{2,1,0:T(8,128)(2,1)}), bf16[8,48,1024]{2,1,0:T(8,128)(2,1)S(1)}, u32[]{:S(2)}, u32[]{:S(2)}) async-start(bf16[8,48,1024]{2,1,0:T(8,128)(2,1)} %get-tuple-element.47.refs_0_), calls=%async_computation | async-start | bytes 1572864 | tf_op jit(solution)/shard_map/all_to_all | solution.py:337
  71.1 17.9 %all-to-all-done = bf16[8,48,1024]{2,1,0:T(8,128)(2,1)S(1)} async-done(((bf16[8,48,1024]{2,1,0:T(8,128)(2,1)}), bf16[8,48,1024]{2,1,0:T(8,128)(2,1)S(1)}, u32[]{:S(2)}, u32[]{:S(2)}) %all-to-all-start) | async-done | bytes 786464 | tf_op jit(solution)/shard_map/all_to_all | solution.py:337
  91.3 4.3 %shard_map.98 = (bf16[256,256]{1,0:T(8,128)(2,1)}, bf16[256,256]{1,0:T(8,128)(2,1)}, bf16[256,256]{1,0:T(8,128)(2,1)}, bf16[256,256]{1,0:T(8,128)(2,1)}) custom-call(s32[7]{0:T(128)} %stack.95.at, bf16[256,1024]{1,0:T(8,128)(2,1)} %bitcast.112, bf16[2,448,1024]{2,1,0:T(8,128)(2,1)} %get-tuple-element.52.refs_1_.refs_5_.refs_2_, ...), custom_call_target="tpu_custom_call" | custom-call | tf_op jit(solution)/shard_map/pallas_call | solution.py:31
  98.0 4.3 %collective-permute-done.12 = bf16[256,256]{1,0:T(8,128)(2,1)S(1)} collective-permute-done((bf16[256,256]{1,0:T(8,128)(2,1)}, bf16[256,256]{1,0:T(8,128)(2,1)S(1)}, u32[]{:S(2)}, u32[]{:S(2)}) %collective-permute-start.12) | collective-permute-done | bytes 131104 | tf_op jit(solution)/shard_map/ppermute | solution.py:47
  103.4 3.6 %shard_map.99 = (f32[4,16,3584]{2,1,0:T(8,128)}, f32[4,128]{1,0:T(4,128)}) custom-call(s32[7]{0:T(128)} %stack.95.at, bf16[512,3584]{1,0:T(8,128)(2,1)} %refs_6_.1, bf16[16,512]{1,0:T(8,128)(2,1)} %get-tuple-element.117.refs_1_), custom_call_target="tpu_custom_call" | custom-call | tf_op jit(solution)/shard_map/pallas_call | solution.py:31
  108.2 3.5 %shard_map.100.refs_4_.refs_2_.refs_5_ = bf16[2,448,1024]{2,1,0:T(8,128)(2,1)} custom-call(s32[7]{0:T(128)} %stack.95.at, bf16[256,256]{1,0:T(8,128)(2,1)} %add_convert_fusion.1.refs_0_, f32[4,128]{1,0:T(4,128)} %get-tuple-element.58.refs_1_.refs_9_, bf16[448,1024]{1,0:T(8,128)(2,1)} %get-tuple-element.49.refs_1_.refs_2_, ...), custom_call_target="tpu_custom_call" | custom-call | tf_op jit(solution)/shard_map/pallas_call | solution.py:31
  113.1 4.4 %all-to-all-start.1 = ((bf16[8,64,1024]{2,1,0:T(8,128)(2,1)}), bf16[8,64,1024]{2,1,0:T(8,128)(2,1)S(1)}, u32[]{:S(2)}, u32[]{:S(2)}) async-start(bf16[8,64,1024]{2,1,0:T(8,128)(2,1)} %get-tuple-element.78), calls=%async_computation.1 | async-start | bytes 2097152 | tf_op jit(solution)/shard_map/all_to_all | solution.py:411
  121.2 3.1 %collective-permute-done.27 = bf16[16,448]{1,0:T(8,128)(2,1)S(1)} collective-permute-done((bf16[16,448]{1,0:T(8,128)(2,1)S(1)}, bf16[16,448]{1,0:T(8,128)(2,1)S(1)}, u32[]{:S(2)}, u32[]{:S(2)}) %collective-permute-start.27) | collective-permute-done | bytes 14368 | tf_op jit(solution)/shard_map/ppermute | solution.py:422
  133.1 3.1 %collective-permute-start.14 = (bf16[256,256]{1,0:T(8,128)(2,1)S(1)}, bf16[256,256]{1,0:T(8,128)(2,1)S(1)}, u32[]{:S(2)}, u32[]{:S(2)}) collective-permute-start(bf16[256,256]{1,0:T(8,128)(2,1)S(1)} %copy-done.4), channel_id=1, source_target_pairs={{0,4},{2,6},{4,0},{6,2},{1,5},{3,7},{5,1},{7,3},{8,12},{10,14},{12... | collective-permute-start | bytes 393224 | tf_op jit(solution)/shard_map/ppermute | solution.py:47
  138.2 3.3 %shard_map.103 = (bf16[32,256]{1,0:T(8,128)(2,1)}, bf16[32,256]{1,0:T(8,128)(2,1)}, bf16[32,256]{1,0:T(8,128)(2,1)}, bf16[32,256]{1,0:T(8,128)(2,1)}) custom-call(s32[7]{0:T(128)} %stack.95.at, bf16[256,256]{1,0:T(8,128)(2,1)} %add_convert_fusion.1.refs_0_, bf16[16,896]{1,0:T(8,128)(2,1)} %pad_maximum_fusion.4.refs_1_, ...), custom_call_target="tpu_custom_call" | custom-call | tf_op jit(solution)/shard_map/pallas_call | solution.py:31
  143.1 3.3 %all-to-all-done.1 = bf16[8,64,1024]{2,1,0:T(8,128)(2,1)S(1)} async-done(((bf16[8,64,1024]{2,1,0:T(8,128)(2,1)}), bf16[8,64,1024]{2,1,0:T(8,128)(2,1)S(1)}, u32[]{:S(2)}, u32[]{:S(2)}) %all-to-all-start.1) | async-done | bytes 1048608 | tf_op jit(solution)/shard_map/all_to_all | solution.py:411
  147.4 6.1 %shard_map.107 = (bf16[512,256]{1,0:T(8,128)(2,1)}, bf16[512,256]{1,0:T(8,128)(2,1)}, bf16[512,256]{1,0:T(8,128)(2,1)}, bf16[512,256]{1,0:T(8,128)(2,1)}) custom-call(s32[7]{0:T(128)} %stack.95.at, bf16[256,256]{1,0:T(8,128)(2,1)} %add_convert_fusion.1.refs_0_, bf16[512,1024]{1,0:T(8,128)(2,1)} %bitcast.108, ...), custom_call_target="tpu_custom_call" | custom-call | tf_op jit(solution)/shard_map/pallas_call | solution.py:31
  157.1 4.5 %collective-permute-done.31 = bf16[32,256]{1,0:T(8,128)(2,1)S(1)} collective-permute-done((bf16[32,256]{1,0:T(8,128)(2,1)S(1)}, bf16[32,256]{1,0:T(8,128)(2,1)S(1)}, u32[]{:S(2)}, u32[]{:S(2)}) %collective-permute-start.31) | collective-permute-done | bytes 16416 | tf_op jit(solution)/shard_map/ppermute | solution.py:47
  162.8 5.5 %collective-permute-done.15.refs_3_ = bf16[256,256]{1,0:T(8,128)(2,1)S(1)} collective-permute-done((bf16[256,256]{1,0:T(8,128)(2,1)S(1)}, bf16[256,256]{1,0:T(8,128)(2,1)S(1)}, u32[]{:S(2)}, u32[]{:S(2)}) %collective-permute-start.15) | collective-permute-done | bytes 131104 | tf_op jit(solution)/shard_map/ppermute | solution.py:47
  169.2 4.5 %shard_map.101 = (bf16[256,256]{1,0:T(8,128)(2,1)}, bf16[256,256]{1,0:T(8,128)(2,1)}, bf16[256,256]{1,0:T(8,128)(2,1)}, bf16[256,256]{1,0:T(8,128)(2,1)}) custom-call(s32[7]{0:T(128)} %stack.95.at, bf16[256,256]{1,0:T(8,128)(2,1)} %add_convert_fusion.1.refs_0_, bf16[256,256]{1,0:T(8,128)(2,1)} %copy-done.27, bf16[256,256]{1,0:T(8,128)(2,1)} %copy-done.28, ...), custom_call_target="tpu_custom_call" | custom-call | tf_op jit(solution)/shard_map/pallas_call | solution.py:31
  178.5 3.0 %collective-permute-done.35.refs_3_ = bf16[32,256]{1,0:T(8,128)(2,1)S(1)} collective-permute-done((bf16[32,256]{1,0:T(8,128)(2,1)S(1)}, bf16[32,256]{1,0:T(8,128)(2,1)S(1)}, u32[]{:S(2)}, u32[]{:S(2)}) %collective-permute-start.35) | collective-permute-done | bytes 16416 | tf_op jit(solution)/shard_map/ppermute | solution.py:47
  191.2 3.4 %shard_map.104.refs_1_ = bf16[48,1024]{1,0:T(8,128)(2,1)} custom-call(s32[7]{0:T(128)} %stack.95.at, bf16[256,256]{1,0:T(8,128)(2,1)} %copy-done.7, bf16[32,256]{1,0:T(8,128)(2,1)} %copy-done.40, bf16[32,256]{1,0:T(8,128)(2,1)} %copy-done.44, bf16[32,256]{1,0:T(8,128)(2,1)} %copy-done.45, bf16[32,256]{1,0:T(8,128)(2,1)} %copy-done.46, ...), custom_call_target="tpu_custom_call" | custom-call | tf_op jit(solution)/shard_map/pallas_call | solution.py:31
  199.1 4.4 %shard_map.108 = (bf16[256,256]{1,0:T(8,128)(2,1)}, bf16[256,256]{1,0:T(8,128)(2,1)}, bf16[256,256]{1,0:T(8,128)(2,1)}, bf16[256,256]{1,0:T(8,128)(2,1)}) custom-call(s32[7]{0:T(128)} %stack.95.at, bf16[256,256]{1,0:T(8,128)(2,1)} %copy-done.7, bf16[256,256]{1,0:T(8,128)(2,1)} %bitcast.122, bf16[256,256]{1,0:T(8,128)(2,1)} %copy-done.31, ...), custom_call_target="tpu_custom_call" | custom-call | tf_op jit(solution)/shard_map/pallas_call | solution.py:31
  211.7 4.4 %shard_map.102 = (bf16[256,256]{1,0:T(8,128)(2,1)}, bf16[256,256]{1,0:T(8,128)(2,1)}, bf16[256,256]{1,0:T(8,128)(2,1)}, bf16[256,256]{1,0:T(8,128)(2,1)}) custom-call(s32[7]{0:T(128)} %stack.95.at, bf16[256,256]{1,0:T(8,128)(2,1)} %copy-done.7, bf16[256,256]{1,0:T(8,128)(2,1)} %copy-done.26, bf16[256,256]{1,0:T(8,128)(2,1)} %copy-done.29, ...), custom_call_target="tpu_custom_call" | custom-call | tf_op jit(solution)/shard_map/pallas_call | solution.py:31
  226.6 6.0 %shard_map.106 = (f32[4,16,3584]{2,1,0:T(8,128)}, f32[4,128]{1,0:T(4,128)}) custom-call(s32[7]{0:T(128)} %stack.95.at, bf16[256,256]{1,0:T(8,128)(2,1)} %get-tuple-element.64.refs_0_, bf16[16,1024]{1,0:T(8,128)(2,1)} %get-tuple-element.70.refs_1_, bf16[16,1024]{1,0:T(8,128)(2,1)} %copy-done.41, bf16[16,1024]{1,0:T(8,128)(2,1)} %copy-done.42, ...), custom_call_target="tpu_custom_call" | custom-call | tf_op jit(solution)/shard_map/pallas_call | solution.py:31
  235.1 3.5 %all-to-all-start.2 = ((f32[32,1,256]{2,1,0:T(1,128)}), f32[32,1,256]{2,1,0:T(1,128)S(1)}, u32[]{:S(2)}, u32[]{:S(2)}) async-start(f32[32,1,256]{2,1,0:T(1,128)} %reshape.146), calls=%async_computation.2 | async-start | bytes 65536 | tf_op jit(solution)/shard_map/all_to_all | solution.py:478
  238.9 6.9 %all-to-all-done.2 = f32[32,1,256]{2,1,0:T(1,128)S(1)} async-done(((f32[32,1,256]{2,1,0:T(1,128)}), f32[32,1,256]{2,1,0:T(1,128)S(1)}, u32[]{:S(2)}, u32[]{:S(2)}) %all-to-all-start.2) | async-done | bytes 32800 | tf_op jit(solution)/shard_map/all_to_all | solution.py:478
  253.8 3.4 %all-to-all-start.3 = ((bf16[8,32,448]{2,1,0:T(8,128)(2,1)}), bf16[8,32,448]{2,1,0:T(8,128)(2,1)S(1)}, u32[]{:S(2)}, u32[]{:S(2)}) async-start(bf16[8,32,448]{2,1,0:T(8,128)(2,1)} %copy.48), calls=%async_computation.3 | async-start | bytes 524288 | tf_op jit(solution)/shard_map/all_to_all | solution.py:487
  257.9 3.1 %collective-permute-start.61 = (f32[16,256]{1,0:T(8,128)S(1)}, f32[16,256]{1,0:T(8,128)S(1)}, u32[]{:S(2)}, u32[]{:S(2)}) collective-permute-start(f32[16,256]{1,0:T(8,128)S(1)} %get-tuple-element.103), channel_id=1, source_target_pairs={{0,25},{1,24},{8,17},{9,16},{16,9},{17,8},{24,1},{25,0},{2,27},{3,... | collective-permute-start | bytes 49160 | tf_op jit(solution)/shard_map/ppermute | solution.py:47
  262.8 3.1 %all-to-all-done.3 = bf16[8,32,448]{2,1,0:T(8,128)(2,1)S(1)} async-done(((bf16[8,32,448]{2,1,0:T(8,128)(2,1)}), bf16[8,32,448]{2,1,0:T(8,128)(2,1)S(1)}, u32[]{:S(2)}, u32[]{:S(2)}) %all-to-all-start.3) | async-done | bytes 229408 | tf_op jit(solution)/shard_map/all_to_all | solution.py:487
  (302 shorter events, 105.7 us)
Async XLA Ops:
  18.7 36.4 %collective-permute-start.6 = (bf16[448,1024]{1,0:T(8,128)(2,1)}, bf16[448,1024]{1,0:T(8,128)(2,1)S(1)}, u32[]{:S(2)}, u32[]{:S(2)}) collective-permute-start(bf16[448,1024]{1,0:T(8,128)(2,1)} %get-tuple-element.46.refs_0_), channel_id=1, source_target_pairs={{8,9},{9,8},{24,25},{25,24},{10,11},{11,10},{26,27},{27,26},{12,13... | collective-permute-start | bytes 2752520 | tf_op jit(solution)/shard_map/ppermute | solution.py:348
  19.4 35.7 %collective-permute-start.7 = (bf16[448,1024]{1,0:T(8,128)(2,1)}, bf16[448,1024]{1,0:T(8,128)(2,1)S(1)}, u32[]{:S(2)}, u32[]{:S(2)}) collective-permute-start(bf16[448,1024]{1,0:T(8,128)(2,1)} %get-tuple-element.50), channel_id=1, source_target_pairs={{8,24},{9,25},{24,8},{25,9},{10,26},{11,27},{26,10},{27,11},{12,28... | collective-permute-start | bytes 2752520 | tf_op jit(solution)/shard_map/ppermute | solution.py:348
  20.1 34.9 %collective-permute-start.8 = (bf16[448,1024]{1,0:T(8,128)(2,1)}, bf16[448,1024]{1,0:T(8,128)(2,1)S(1)}, u32[]{:S(2)}, u32[]{:S(2)}) collective-permute-start(bf16[448,1024]{1,0:T(8,128)(2,1)} %get-tuple-element.51), channel_id=1, source_target_pairs={{8,25},{9,24},{24,9},{25,8},{10,27},{11,26},{26,11},{27,10},{12,29... | collective-permute-start | bytes 2752520 | tf_op jit(solution)/shard_map/ppermute | solution.py:348
  27.4 16.5 %collective-permute-start.4 = (bf16[16,4480]{1,0:T(8,128)(2,1)S(1)}, bf16[16,4480]{1,0:T(8,128)(2,1)S(1)}, u32[]{:S(2)}, u32[]{:S(2)}) collective-permute-start(bf16[16,4480]{1,0:T(8,128)(2,1)S(1)} %pad_maximum_fusion.1.refs_1_), channel_id=1, source_target_pairs={{0,16},{8,24},{16,0},{24,8},{1,17},{9,25},{17,1},{25,9},{2,18},{10... | collective-permute-start | bytes 430088 | tf_op jit(solution)/shard_map/ppermute | solution.py:47
  28.4 24.1 %collective-permute-start.5 = (bf16[16,4480]{1,0:T(8,128)(2,1)S(1)}, bf16[16,4480]{1,0:T(8,128)(2,1)S(1)}, u32[]{:S(2)}, u32[]{:S(2)}) collective-permute-start(bf16[16,4480]{1,0:T(8,128)(2,1)S(1)} %pad_maximum_fusion.1.refs_1_), channel_id=1, source_target_pairs={{0,24},{8,16},{16,8},{24,0},{1,25},{9,17},{17,9},{25,1},{2,26},{10... | collective-permute-start | bytes 430088 | tf_op jit(solution)/shard_map/ppermute | solution.py:47
  60.8 29.2 %collective-permute-start.9 = (bf16[2,448,1024]{2,1,0:T(8,128)(2,1)}, bf16[2,448,1024]{2,1,0:T(8,128)(2,1)S(1)}, u32[]{:S(2)}, u32[]{:S(2)}) collective-permute-start(bf16[2,448,1024]{2,1,0:T(8,128)(2,1)} %get-tuple-element.52.refs_1_.refs_5_.refs_2_), channel_id=1, source_target_pairs={{8,0},{9,1},{10,2},{11,3},{12,4},{13,5},{14,6},{15,7},{24,16},{25,... | collective-permute-start | bytes 5505032 | tf_op jit(solution)/shard_map/ppermute | solution.py:368
  62.1 27.0 %all-to-all-start = ((bf16[8,48,1024]{2,1,0:T(8,128)(2,1)}), bf16[8,48,1024]{2,1,0:T(8,128)(2,1)S(1)}, u32[]{:S(2)}, u32[]{:S(2)}) async-start(bf16[8,48,1024]{2,1,0:T(8,128)(2,1)} %get-tuple-element.47.refs_0_), calls=%async_computation | async-start | bytes 1572864 | tf_op jit(solution)/shard_map/all_to_all | solution.py:337
  67.0 41.2 %collective-permute-start.16 = (bf16[448,1024]{1,0:T(8,128)(2,1)}, bf16[448,1024]{1,0:T(8,128)(2,1)}, u32[]{:S(2)}, u32[]{:S(2)}) collective-permute-start(bf16[448,1024]{1,0:T(8,128)(2,1)} %get-tuple-element.46.refs_0_), channel_id=1, source_target_pairs={{16,17},{17,16},{18,19},{19,18},{20,21},{21,20},{22,23},{23,22}} | collective-permute-start | bytes 2752520 | tf_op jit(solution)/shard_map/ppermute | solution.py:348
  68.6 39.6 %collective-permute-start.17 = (bf16[448,1024]{1,0:T(8,128)(2,1)}, bf16[448,1024]{1,0:T(8,128)(2,1)}, u32[]{:S(2)}, u32[]{:S(2)}) collective-permute-start(bf16[448,1024]{1,0:T(8,128)(2,1)} %get-tuple-element.50), channel_id=1, source_target_pairs={{16,0},{17,1},{18,2},{19,3},{20,4},{21,5},{22,6},{23,7}} | collective-permute-start | bytes 2752520 | tf_op jit(solution)/shard_map/ppermute | solution.py:348
  69.8 38.4 %collective-permute-start.18 = (bf16[448,1024]{1,0:T(8,128)(2,1)}, bf16[448,1024]{1,0:T(8,128)(2,1)}, u32[]{:S(2)}, u32[]{:S(2)}) collective-permute-start(bf16[448,1024]{1,0:T(8,128)(2,1)} %get-tuple-element.51), channel_id=1, source_target_pairs={{16,1},{17,0},{18,3},{19,2},{20,5},{21,4},{22,7},{23,6}} | collective-permute-start | bytes 2752520 | tf_op jit(solution)/shard_map/ppermute | solution.py:348
  111.7 25.2 %collective-permute-start.19 = (bf16[2,448,1024]{2,1,0:T(8,128)(2,1)}, bf16[2,448,1024]{2,1,0:T(8,128)(2,1)S(1)}, u32[]{:S(2)}, u32[]{:S(2)}) collective-permute-start(bf16[2,448,1024]{2,1,0:T(8,128)(2,1)} %shard_map.100.refs_4_.refs_2_.refs_5_), channel_id=1, source_target_pairs={{0,8},{1,9},{2,10},{3,11},{4,12},{5,13},{6,14},{7,15},{16,24},{17,... | collective-permute-start | bytes 5505032 | tf_op jit(solution)/shard_map/ppermute | solution.py:368
  113.1 33.2 %all-to-all-start.1 = ((bf16[8,64,1024]{2,1,0:T(8,128)(2,1)}), bf16[8,64,1024]{2,1,0:T(8,128)(2,1)S(1)}, u32[]{:S(2)}, u32[]{:S(2)}) async-start(bf16[8,64,1024]{2,1,0:T(8,128)(2,1)} %get-tuple-element.78), calls=%async_computation.1 | async-start | bytes 2097152 | tf_op jit(solution)/shard_map/all_to_all | solution.py:411
  117.5 86.0 %collective-permute-start.26 = (bf16[2,448,1024]{2,1,0:T(8,128)(2,1)}, bf16[2,448,1024]{2,1,0:T(8,128)(2,1)}, u32[]{:S(2)}, u32[]{:S(2)}) collective-permute-start(bf16[2,448,1024]{2,1,0:T(8,128)(2,1)} %get-tuple-element.63.refs_4_), channel_id=1, source_target_pairs={{8,0},{9,1},{10,2},{11,3},{12,4},{13,5},{14,6},{15,7},{24,16},{25,... | collective-permute-start | bytes 5505032 | tf_op jit(solution)/shard_map/ppermute | solution.py:368
  131.6 21.9 %collective-permute-start.13 = (bf16[256,256]{1,0:T(8,128)(2,1)S(1)}, bf16[256,256]{1,0:T(8,128)(2,1)S(1)}, u32[]{:S(2)}, u32[]{:S(2)}) collective-permute-start(bf16[256,256]{1,0:T(8,128)(2,1)S(1)} %copy-done.4), channel_id=1, source_target_pairs={{0,2},{2,0},{4,6},{6,4},{1,3},{3,1},{5,7},{7,5},{8,10},{10,8},{12,... | collective-permute-start | bytes 393224 | tf_op jit(solution)/shard_map/ppermute | solution.py:47
  133.1 21.7 %collective-permute-start.14 = (bf16[256,256]{1,0:T(8,128)(2,1)S(1)}, bf16[256,256]{1,0:T(8,128)(2,1)S(1)}, u32[]{:S(2)}, u32[]{:S(2)}) collective-permute-start(bf16[256,256]{1,0:T(8,128)(2,1)S(1)} %copy-done.4), channel_id=1, source_target_pairs={{0,4},{2,6},{4,0},{6,2},{1,5},{3,7},{5,1},{7,3},{8,12},{10,14},{12... | collective-permute-start | bytes 393224 | tf_op jit(solution)/shard_map/ppermute | solution.py:47
  141.5 15.2 %collective-permute-start.33 = (bf16[32,256]{1,0:T(8,128)(2,1)}, bf16[32,256]{1,0:T(8,128)(2,1)S(1)}, u32[]{:S(2)}, u32[]{:S(2)}) collective-permute-start(bf16[32,256]{1,0:T(8,128)(2,1)} %get-tuple-element.69), channel_id=1, source_target_pairs={{0,6},{2,4},{4,2},{6,0},{1,7},{3,5},{5,3},{7,1},{8,14},{10,12},{12... | collective-permute-start | bytes 49160 | tf_op jit(solution)/shard_map/ppermute | solution.py:47
  141.5 15.5 %collective-permute-start.32 = (bf16[32,256]{1,0:T(8,128)(2,1)}, bf16[32,256]{1,0:T(8,128)(2,1)S(1)}, u32[]{:S(2)}, u32[]{:S(2)}) collective-permute-start(bf16[32,256]{1,0:T(8,128)(2,1)} %get-tuple-element.68), channel_id=1, source_target_pairs={{0,4},{2,6},{4,0},{6,2},{1,5},{3,7},{5,1},{7,3},{8,12},{10,14},{12... | collective-permute-start | bytes 49160 | tf_op jit(solution)/shard_map/ppermute | solution.py:47
  153.5 20.1 %collective-permute-start.48 = (bf16[512,256]{1,0:T(8,128)(2,1)}, bf16[512,256]{1,0:T(8,128)(2,1)S(1)}, u32[]{:S(2)}, u32[]{:S(2)}) collective-permute-start(bf16[512,256]{1,0:T(8,128)(2,1)} %get-tuple-element.82), channel_id=1, source_target_pairs={{0,17},{1,16},{16,1},{17,0},{2,19},{3,18},{18,3},{19,2},{4,21},{5,... | collective-permute-start | bytes 786440 | tf_op jit(solution)/shard_map/ppermute | solution.py:47
  154.9 20.0 %collective-permute-start.47 = (bf16[512,256]{1,0:T(8,128)(2,1)}, bf16[512,256]{1,0:T(8,128)(2,1)S(1)}, u32[]{:S(2)}, u32[]{:S(2)}) collective-permute-start(bf16[512,256]{1,0:T(8,128)(2,1)} %get-tuple-element.81), channel_id=1, source_target_pairs={{0,16},{1,17},{16,0},{17,1},{2,18},{3,19},{18,2},{19,3},{4,20},{5,... | collective-permute-start | bytes 786440 | tf_op jit(solution)/shard_map/ppermute | solution.py:47
  156.6 19.7 %collective-permute-start.46 = (bf16[512,256]{1,0:T(8,128)(2,1)}, bf16[512,256]{1,0:T(8,128)(2,1)S(1)}, u32[]{:S(2)}, u32[]{:S(2)}) collective-permute-start(bf16[512,256]{1,0:T(8,128)(2,1)} %get-tuple-element.80), channel_id=1, source_target_pairs={{0,1},{1,0},{16,17},{17,16},{2,3},{3,2},{18,19},{19,18},{4,5},{5,4... | collective-permute-start | bytes 786440 | tf_op jit(solution)/shard_map/ppermute | solution.py:47
  181.5 13.0 %collective-permute-start.49 = (bf16[256,256]{1,0:T(8,128)(2,1)S(1)}, bf16[256,256]{1,0:T(8,128)(2,1)S(1)}, u32[]{:S(2)}, u32[]{:S(2)}) collective-permute-start(bf16[256,256]{1,0:T(8,128)(2,1)S(1)} %bitcast.119), channel_id=1, source_target_pairs={{0,2},{2,0},{4,6},{6,4},{1,3},{3,1},{5,7},{7,5},{8,10},{10,8},{12,... | collective-permute-start | bytes 393224 | tf_op jit(solution)/shard_map/ppermute | solution.py:47
  181.5 13.9 %collective-permute-start.50 = (bf16[256,256]{1,0:T(8,128)(2,1)S(1)}, bf16[256,256]{1,0:T(8,128)(2,1)S(1)}, u32[]{:S(2)}, u32[]{:S(2)}) collective-permute-start(bf16[256,256]{1,0:T(8,128)(2,1)S(1)} %bitcast.120), channel_id=1, source_target_pairs={{0,4},{2,6},{4,0},{6,2},{1,5},{3,7},{5,1},{7,3},{8,12},{10,14},{12... | collective-permute-start | bytes 393224 | tf_op jit(solution)/shard_map/ppermute | solution.py:47
  182.9 15.6 %collective-permute-start.51 = (bf16[256,256]{1,0:T(8,128)(2,1)S(1)}, bf16[256,256]{1,0:T(8,128)(2,1)S(1)}, u32[]{:S(2)}, u32[]{:S(2)}) collective-permute-start(bf16[256,256]{1,0:T(8,128)(2,1)S(1)} %bitcast.121), channel_id=1, source_target_pairs={{0,6},{2,4},{4,2},{6,0},{1,7},{3,5},{5,3},{7,1},{8,14},{10,12},{12... | collective-permute-start | bytes 393224 | tf_op jit(solution)/shard_map/ppermute | solution.py:47
  190.6 18.1 %collective-permute-start.23 = (bf16[256,256]{1,0:T(8,128)(2,1)S(1)}, bf16[256,256]{1,0:T(8,128)(2,1)S(1)}, u32[]{:S(2)}, u32[]{:S(2)}) collective-permute-start(bf16[256,256]{1,0:T(8,128)(2,1)S(1)} %add_convert_fusion.refs_0_), channel_id=1, source_target_pairs={{0,2},{2,0},{4,6},{6,4},{1,3},{3,1},{5,7},{7,5},{8,10},{10,8},{12,... | collective-permute-start | bytes 393224 | tf_op jit(solution)/shard_map/ppermute | solution.py:47
  194.6 14.7 %collective-permute-start.24 = (bf16[256,256]{1,0:T(8,128)(2,1)}, bf16[256,256]{1,0:T(8,128)(2,1)S(1)}, u32[]{:S(2)}, u32[]{:S(2)}) collective-permute-start(bf16[256,256]{1,0:T(8,128)(2,1)} %copy-done.7), channel_id=1, source_target_pairs={{0,4},{2,6},{4,0},{6,2},{1,5},{3,7},{5,1},{7,3},{8,12},{10,14},{12... | collective-permute-start | bytes 393224 | tf_op jit(solution)/shard_map/ppermute | solution.py:47
  195.4 13.9 %collective-permute-start.25 = (bf16[256,256]{1,0:T(8,128)(2,1)}, bf16[256,256]{1,0:T(8,128)(2,1)S(1)}, u32[]{:S(2)}, u32[]{:S(2)}) collective-permute-start(bf16[256,256]{1,0:T(8,128)(2,1)} %copy-done.7), channel_id=1, source_target_pairs={{0,6},{2,4},{4,2},{6,0},{1,7},{3,5},{5,3},{7,1},{8,14},{10,12},{12... | collective-permute-start | bytes 393224 | tf_op jit(solution)/shard_map/ppermute | solution.py:47
  203.5 17.4 %collective-permute-start.54 = (bf16[256,256]{1,0:T(8,128)(2,1)}, bf16[256,256]{1,0:T(8,128)(2,1)S(1)}, u32[]{:S(2)}, u32[]{:S(2)}) collective-permute-start(bf16[256,256]{1,0:T(8,128)(2,1)} %get-tuple-element.86), channel_id=1, source_target_pairs={{0,17},{1,16},{16,1},{17,0},{2,19},{3,18},{18,3},{19,2},{4,21},{5,... | collective-permute-start | bytes 393224 | tf_op jit(solution)/shard_map/ppermute | solution.py:47
  207.3 14.8 %collective-permute-start.53 = (bf16[256,256]{1,0:T(8,128)(2,1)}, bf16[256,256]{1,0:T(8,128)(2,1)S(1)}, u32[]{:S(2)}, u32[]{:S(2)}) collective-permute-start(bf16[256,256]{1,0:T(8,128)(2,1)} %get-tuple-element.85), channel_id=1, source_target_pairs={{0,16},{1,17},{16,0},{17,1},{2,18},{3,19},{18,2},{19,3},{4,20},{5,... | collective-permute-start | bytes 393224 | tf_op jit(solution)/shard_map/ppermute | solution.py:47
  208.7 13.4 %collective-permute-start.52 = (bf16[256,256]{1,0:T(8,128)(2,1)}, bf16[256,256]{1,0:T(8,128)(2,1)S(1)}, u32[]{:S(2)}, u32[]{:S(2)}) collective-permute-start(bf16[256,256]{1,0:T(8,128)(2,1)} %get-tuple-element.84), channel_id=1, source_target_pairs={{0,1},{1,0},{16,17},{17,16},{2,3},{3,2},{18,19},{19,18},{4,5},{5,4... | collective-permute-start | bytes 393224 | tf_op jit(solution)/shard_map/ppermute | solution.py:47
  222.5 11.2 %collective-permute-start.45 = (bf16[256,256]{1,0:T(8,128)(2,1)}, bf16[256,256]{1,0:T(8,128)(2,1)S(1)}, u32[]{:S(2)}, u32[]{:S(2)}) collective-permute-start(bf16[256,256]{1,0:T(8,128)(2,1)} %get-tuple-element.77), channel_id=1, source_target_pairs={{0,17},{1,16},{16,1},{17,0},{2,19},{3,18},{18,3},{19,2},{4,21},{5,... | collective-permute-start | bytes 393224 | tf_op jit(solution)/shard_map/ppermute | solution.py:47
  248.8 12.2 %collective-permute-start.57 = (f32[16,256]{1,0:T(8,128)S(1)}, f32[16,256]{1,0:T(8,128)S(1)}, u32[]{:S(2)}, u32[]{:S(2)}) collective-permute-start(f32[16,256]{1,0:T(8,128)S(1)} %get-tuple-element.107), channel_id=1, source_target_pairs={{0,9},{1,8},{8,1},{9,0},{16,25},{17,24},{24,17},{25,16},{2,11},{3,... | collective-permute-start | bytes 49160 | tf_op jit(solution)/shard_map/ppermute | solution.py:47
  253.8 12.2 %all-to-all-start.3 = ((bf16[8,32,448]{2,1,0:T(8,128)(2,1)}), bf16[8,32,448]{2,1,0:T(8,128)(2,1)S(1)}, u32[]{:S(2)}, u32[]{:S(2)}) async-start(bf16[8,32,448]{2,1,0:T(8,128)(2,1)} %copy.48), calls=%async_computation.3 | async-start | bytes 524288 | tf_op jit(solution)/shard_map/all_to_all | solution.py:487
  (84 other events, 683.2 us)
